TPU v7x, 32 devices: a 4x4x1 block of a 4x4x8 slice. The times are simulated.
32 devices in a mesh: dp: 1 (over z), fsdp: 32 (over y, x, core).
Axes of the slice: x: 4, y: 4, z: 1, core: 2. Of those that a mesh axis runs over, the one named last changes fastest.
The devices are a block of a 4x4x8 slice.
Arguments:
- hidden: bfloat16 [32, 1024, 2048], P(('dp', 'fsdp'))
- g_attn: bfloat16 [2048], P('fsdp')
- w_query: bfloat16 [2048, 2048], P('fsdp')
- w_key: bfloat16 [2048, 512], P('fsdp')
- w_value: bfloat16 [2048, 512], P('fsdp')
- w_out: bfloat16 [2048, 2048], P('fsdp')
- g_mlp: bfloat16 [2048], P('fsdp')
- w_gate: bfloat16 [2048, 8192], P('fsdp')
- w_up: bfloat16 [2048, 8192], P('fsdp')
- w_down: bfloat16 [8192, 2048], P('fsdp')
- cos_tab: float32 [1024, 32], replicated
- sin_tab: float32 [1024, 32], replicated
Outputs:
- output 1: bfloat16 [32, 1024, 2048], P(('dp', 'fsdp'))
- output 2: bfloat16 [32, 1024, 8, 64], P(('dp', 'fsdp'))
- output 3: bfloat16 [32, 1024, 8, 64], P(('dp', 'fsdp'))
All inputs are finite; a program needn't handle non-finite values.
Results may differ from a plain program's by a relative error of at most 0.0190543.
Values are sent between devices in bfloat16 or wider.
A program may use at most 768 MiB of HBM per device.

v0:
```python
import functools
import jax
import jax.numpy as jnp
from jax import lax
from jax.sharding import PartitionSpec as P

NORM_EPS = 1e-5
QUERY_BLOCK = 256


def rms_norm(rows_in, gain_vec):
    upcast = rows_in.astype(jnp.float32)
    scaled = upcast * lax.rsqrt(jnp.mean(upcast * upcast, axis=-1, keepdims=True) + NORM_EPS)
    return (scaled * gain_vec.astype(jnp.float32)).astype(jnp.bfloat16)


def apply_rope(heads_in, cos_tab, sin_tab):
    half_dim = cos_tab.shape[-1]
    upcast = heads_in.astype(jnp.float32)
    lo_half = upcast[..., :half_dim]
    hi_half = upcast[..., half_dim:]
    cos_bc = cos_tab[:, None, :]
    sin_bc = sin_tab[:, None, :]
    rotated = jnp.concatenate([lo_half * cos_bc - hi_half * sin_bc, hi_half * cos_bc + lo_half * sin_bc], axis=-1)
    return rotated.astype(jnp.bfloat16)


def causal_attention(query_grp, key_rot, value_heads):
    seq_len = query_grp.shape[1]
    head_dim = query_grp.shape[-1]
    blk_len = min(QUERY_BLOCK, seq_len)
    out_blocks = []
    for blk_start in range(0, seq_len, blk_len):
        blk_stop = blk_start + blk_len
        scores = jnp.einsum("bqkgd,bskd->bkgqs", query_grp[:, blk_start:blk_stop], key_rot[:, :blk_stop], preferred_element_type=jnp.float32) * head_dim ** -0.5
        allowed = (blk_start + jnp.arange(blk_len))[:, None] >= jnp.arange(blk_stop)[None, :]
        scores = jnp.where(allowed, scores, -jnp.inf)
        prob_bf16 = jax.nn.softmax(scores, axis=-1).astype(jnp.bfloat16)
        out_blocks.append(jnp.einsum("bkgqs,bskd->bqkgd", prob_bf16, value_heads[:, :blk_stop], preferred_element_type=jnp.float32).astype(jnp.bfloat16))
    return jnp.concatenate(out_blocks, axis=1)


def decoder_layer(hidden, g_attn, w_query, w_key, w_value, w_out, g_mlp, w_gate, w_up, w_down, cos_tab, sin_tab):
    num_seqs = hidden.shape[0]
    seq_len = hidden.shape[1]
    head_dim = 2 * cos_tab.shape[1]
    num_heads = w_query.shape[1] // head_dim
    kv_heads = w_key.shape[1] // head_dim
    normed = rms_norm(hidden, g_attn)
    query_proj = jnp.dot(normed, w_query, preferred_element_type=jnp.float32).astype(jnp.bfloat16)
    key_proj = jnp.dot(normed, w_key, preferred_element_type=jnp.float32).astype(jnp.bfloat16)
    value_proj = jnp.dot(normed, w_value, preferred_element_type=jnp.float32).astype(jnp.bfloat16)
    query_rot = apply_rope(query_proj.reshape(num_seqs, seq_len, num_heads, head_dim), cos_tab, sin_tab)
    key_rot = apply_rope(key_proj.reshape(num_seqs, seq_len, kv_heads, head_dim), cos_tab, sin_tab)
    value_heads = value_proj.reshape(num_seqs, seq_len, kv_heads, head_dim)
    query_grp = query_rot.reshape(num_seqs, seq_len, kv_heads, num_heads // kv_heads, head_dim)
    attn_heads = causal_attention(query_grp, key_rot, value_heads)
    attn_flat = attn_heads.reshape(num_seqs, seq_len, num_heads * head_dim)
    attn_proj = jnp.dot(attn_flat, w_out, preferred_element_type=jnp.float32).astype(jnp.bfloat16)
    residual = (hidden.astype(jnp.float32) + attn_proj.astype(jnp.float32)).astype(jnp.bfloat16)
    normed_mlp = rms_norm(residual, g_mlp)
    gate_proj = jnp.dot(normed_mlp, w_gate, preferred_element_type=jnp.float32).astype(jnp.bfloat16)
    up_proj = jnp.dot(normed_mlp, w_up, preferred_element_type=jnp.float32).astype(jnp.bfloat16)
    act_in = (jax.nn.silu(gate_proj.astype(jnp.float32)) * up_proj.astype(jnp.float32)).astype(jnp.bfloat16)
    mlp_out = jnp.dot(act_in, w_down, preferred_element_type=jnp.float32).astype(jnp.bfloat16)
    out_hidden = (residual.astype(jnp.float32) + mlp_out.astype(jnp.float32)).astype(jnp.bfloat16)
    return out_hidden, key_rot, value_heads


def solution(mesh):
    tok_spec = P(("dp", "fsdp"), None, None)
    cache_spec = P(("dp", "fsdp"), None, None, None)
    row_spec = P("fsdp", None)
    gain_spec = P("fsdp")
    table_spec = P(None, None)
    gather_rows = functools.partial(lax.all_gather, axis_name="fsdp", axis=0, tiled=True)

    def local_layer(hidden, g_attn, w_query, w_key, w_value, w_out, g_mlp, w_gate, w_up, w_down, cos_tab, sin_tab):
        return decoder_layer(hidden, gather_rows(g_attn), gather_rows(w_query), gather_rows(w_key), gather_rows(w_value), gather_rows(w_out), gather_rows(g_mlp), gather_rows(w_gate), gather_rows(w_up), gather_rows(w_down), cos_tab, sin_tab)

    return jax.shard_map(local_layer, mesh=mesh, in_specs=(tok_spec, gain_spec, row_spec, row_spec, row_spec, row_spec, gain_spec, row_spec, row_spec, row_spec, table_spec, table_spec), out_specs=(tok_spec, cache_spec, cache_spec), check_vma=False)
```

profile of v0, /device:TPU:97, one launch (start us, length us, event | category | flops | bytes accessed | tf_op | source)
XLA Modules:
  0.0 573.7 jit_solution(17448478803694566888)
XLA Ops:
  7.2 0.7 all-gather.10.cloned.1.call-update
  8.0 0.7 all-gather.8.cloned.1.call-update
  8.8 0.7 all-gather.12.cloned.1.call-update
  9.6 0.6 all-gather.14.cloned.1.call-update
  10.3 0.6 all-gather.16.cloned.1.call-update
  10.9 0.6 all-gather.18.cloned.1.call-update
  11.5 0.1 all-gather.20.cloned.1.call-start
  11.6 0.7 all-gather.20.cloned.1.call-update
  12.3 0.9 dynamic-update-slice
  13.2 0.8 dynamic-update-slice.1
  14.0 50.1 %all-reduce.2 = (bf16[2048]{0:T(1024)(128)(2,1)S(1)}, bf16[2048]{0:T(1024)(128)(2,1)S(1)}) all-reduce(bf16[2048]{0:T(1024)(128)(2,1)S(1)} %dynamic-update-slice, bf16[2048]{0:T(1024)(128)(2,1)S(1)} %dynamic-update-slice.1), channel_id=1, replica_groups=mesh['dp'=1,'fsdp'=32] {'fsdp'}, use_global_device_ids=true, to_apply=%add | all-reduce | flops 4096 | bytes 16384
  64.2 0.6 convert_element_type.205
  64.8 3.1 fusion.17
  67.9 0.1 iota_compare_fusion.2
  68.0 0.1 iota_compare_fusion.1
  68.1 0.2 iota_compare_fusion
  68.4 5.4 convolution_convert_fusion
  73.8 0.2 convert.26
  74.0 0.3 subtract_convert_fusion.1
  74.4 1.1 pad_maximum_fusion.1
  75.5 17.0 %all-gather.8.cloned.1.call-done = bf16[2048,512]{1,0:T(8,128)(2,1)} async-done(((bf16[64,512]{1,0:T(8,128)(2,1)}), bf16[2048,512]{1,0:T(8,128)(2,1)}) %all-gather.8.cloned.1.call-update) | async-done | bytes 2097168 | tf_op jit(solution)/shard_map/all_gather | solution.py:79
  92.5 5.3 convolution_convert_fusion.1
  97.9 43.3 %all-gather.12.cloned.1.call-done = bf16[2048,2048]{1,0:T(8,128)(2,1)} async-done(((bf16[64,2048]{1,0:T(8,128)(2,1)}), bf16[2048,2048]{1,0:T(8,128)(2,1)}) %all-gather.12.cloned.1.call-update) | async-done | bytes 8388624 | tf_op jit(solution)/shard_map/all_gather | solution.py:79
  141.2 14.6 %convert_convert_fusion = f32[1024,2048]{1,0:T(8,128)} fusion(bf16[2048,2048]{1,0:T(8,128)(2,1)} %all-gather.12.cloned.1.call-done, bf16[1,1024,2048]{2,1,0:T(8,128)(2,1)} %param.12, f32[2048]{0:T(1024)S(1)} %convert_element_type.175, f32[1024]{0:T(1024)S(1)} %add_rsqrt_fusion.1), kind=kOutput, calls=%fused_computation.61 | convolution fusion | flops 8602517504 | bytes 20983808 | tf_op jit(solution)/shard_map/dot_general | solution.py:50
  155.8 9.5 %copy.23 = f32[1024,2048]{0,1:T(8,128)} copy(f32[1024,2048]{1,0:T(8,128)} %convert_convert_fusion) | data formatting | bytes 16777216 | tf_op jit(solution)/shard_map/convert_element_type | solution.py:19
  165.3 4.9 subtract_convert_fusion
  170.2 1.3 fusion.28
  171.6 3.2 copy-done
  174.8 1.8 fusion.27
  176.5 7.1 %fusion.14 = (f32[8,4,256]{2,1,0:T(4,128)S(1)}, f32[8,512,256,4]{2,1,3,0:T(8,128)}) fusion(pred[256,512]{0,1:T(8,128)(4,1)S(1)} %iota_compare_fusion.2, bf16[1,1024,8,4,32]{1,4,3,2,0:T(8,128)(2,1)S(1)} %bitcast.225, bf16[1,1024,8,4,32]{1,4,3,2,0:T(8,128)(2,1)S(1)} %bitcast.229, bf16[1,1024,8,32]{1,3,2,0:T(8,128)(2,1)S(1)} %get-tuple-element.7, ...), kind=kOutput, calls=%fused_computation.24 | convolution fusion | flops 552591360 | bytes 22183936 | tf_op jit(solution)/shard_map/bqkgd,bskd->bkgqs/dot_general | solution.py:35
  183.7 10.2 %fusion.8 = (f32[8,4,256]{2,1,0:T(4,128)S(1)}, f32[8,768,256,4]{2,1,3,0:T(8,128)}) fusion(pred[256,768]{0,1:T(8,128)(4,1)S(1)} %iota_compare_fusion.1, bf16[1,1024,8,4,32]{1,4,3,2,0:T(8,128)(2,1)S(1)} %bitcast.226, bf16[1,1024,8,4,32]{1,4,3,2,0:T(8,128)(2,1)S(1)} %bitcast.230, bf16[1,1024,8,32]{1,3,2,0:T(8,128)(2,1)S(1)} %get-tuple-element.7, ...), kind=kOutput, calls=%fused_computation.16 | convolution fusion | flops 827842560 | bytes 30638080 | tf_op jit(solution)/shard_map/bqkgd,bskd->bkgqs/dot_general | solution.py:35
  193.9 13.6 %fusion.6 = (f32[8,4,256]{2,1,0:T(4,128)S(1)}, f32[8,1024,256,4]{2,1,3,0:T(8,128)}) fusion(pred[256,1024]{0,1:T(8,128)(4,1)S(1)} %iota_compare_fusion, bf16[1,1024,8,4,32]{1,4,3,2,0:T(8,128)(2,1)S(1)} %bitcast.231, bf16[1,1024,8,4,32]{1,4,3,2,0:T(8,128)(2,1)S(1)} %bitcast.227, bf16[1024,8,32]{0,2,1:T(8,128)(2,1)S(1)} %bitcast.233, ...), kind=kOutput, calls=%fused_computation.11 | convolution fusion | flops 1103093760 | bytes 39092224 | tf_op jit(solution)/shard_map/bqkgd,bskd->bkgqs/dot_general | solution.py:35
  207.5 9.4 %fusion.13 = f32[8,4,256]{2,1,0:T(4,128)S(1)} fusion(f32[8,512,256,4]{2,1,3,0:T(8,128)} %get-tuple-element.14, f32[8,4,256]{2,1,0:T(4,128)S(1)} %get-tuple-element.13, pred[256,512]{0,1:T(8,128)(4,1)S(1)} %iota_compare_fusion.2), kind=kLoop, calls=%fused_computation.23 | loop fusion | flops 16769024 | bytes 16973824 | tf_op jit(solution)/shard_map/reduce_sum | solution.py:38
  216.9 6.7 %fusion.48 = bf16[1,256,8,4,64]{1,4,3,2,0:T(8,128)(2,1)} fusion(f32[8,4,256]{2,1,0:T(4,128)S(1)} %fusion.27, f32[8,4,256]{2,1,0:T(4,128)S(1)} %get-tuple-element.15, f32[8,256,256,4]{2,1,3,0:T(8,128)} %copy-done, pred[256,256]{0,1:T(8,128)(4,1)S(1)} %iota_compare_fusion.3, bf16[1,1024,8,64]{1,3,2,0:T(8,128)(2,1)S(1)} %bitcast.236), kind=kOutput, calls=%fused_computation.76 | convolution fusion | flops 279445504 | bytes 9830400 | tf_op jit(solution)/shard_map/bkgqs,bskd->bqkgd/dot_general | solution.py:39
  223.6 13.5 %fusion.7 = f32[8,4,256]{2,1,0:T(4,128)S(1)} fusion(f32[8,768,256,4]{2,1,3,0:T(8,128)} %get-tuple-element.12, f32[8,4,256]{2,1,0:T(4,128)S(1)} %get-tuple-element.11, pred[256,768]{0,1:T(8,128)(4,1)S(1)} %iota_compare_fusion.1), kind=kLoop, calls=%fused_computation.15 | loop fusion | flops 25157632 | bytes 25427968 | tf_op jit(solution)/shard_map/reduce_sum | solution.py:38
  237.2 0.6 slice-done.7
  237.8 7.4 %fusion.5 = f32[8,4,256]{2,1,0:T(4,128)S(1)} fusion(f32[8,1024,256,4]{2,1,3,0:T(8,128)S(1)} %bitcast.222, f32[8,4,256]{2,1,0:T(4,128)S(1)} %get-tuple-element.9, pred[256,1024]{0,1:T(8,128)(4,1)S(1)} %iota_compare_fusion), kind=kLoop, calls=%fused_computation.10 | loop fusion | flops 33546240 | bytes 33882112 | tf_op jit(solution)/shard_map/reduce_sum | solution.py:38
  245.2 8.1 %fusion.57 = bf16[1,256,8,4,64]{1,4,3,2,0:T(8,128)(2,1)S(1)} fusion(f32[8,4,256]{2,1,0:T(4,128)S(1)} %fusion.13, f32[8,4,256]{2,1,0:T(4,128)S(1)} %get-tuple-element.13, f32[8,512,256,4]{2,1,3,0:T(8,128)} %get-tuple-element.14, pred[256,512]{0,1:T(8,128)(4,1)S(1)} %iota_compare_fusion.2, bf16[1,1024,8,64]{1,3,2,0:T(8,128)(2,1)S(1)} %bitcast.237), kind=kOutput, calls=%fused_computation.79 | convolution fusion | flops 558366720 | bytes 18546688 | tf_op jit(solution)/shard_map/bkgqs,bskd->bqkgd/dot_general | solution.py:39
  253.4 11.6 %fusion.54 = bf16[1,256,8,4,64]{1,4,3,2,0:T(8,128)(2,1)S(1)} fusion(f32[8,4,256]{2,1,0:T(4,128)S(1)} %fusion.7, f32[8,4,256]{2,1,0:T(4,128)S(1)} %get-tuple-element.11, f32[8,768,256,4]{2,1,3,0:T(8,128)} %get-tuple-element.12, pred[256,768]{0,1:T(8,128)(4,1)S(1)} %iota_compare_fusion.1, bf16[1,1024,8,64]{1,3,2,0:T(8,128)(2,1)S(1)} %bitcast.238), kind=kOutput, calls=%fused_computation.78 | convolution fusion | flops 837287936 | bytes 27262976 | tf_op jit(solution)/shard_map/bkgqs,bskd->bqkgd/dot_general | solution.py:39
  265.0 14.1 %fusion.51 = bf16[1,256,8,4,64]{1,4,3,2,0:T(8,128)(2,1)S(1)} fusion(bf16[1024,8,64,1]{0,2,3,1:T(8,128)(2,1)S(1)} %bitcast.239, f32[8,4,256]{2,1,0:T(4,128)S(1)} %fusion.5, f32[8,4,256]{2,1,0:T(4,128)S(1)} %get-tuple-element.9, f32[8,1024,256,4]{2,1,3,0:T(8,128)} %get-tuple-element.10, pred[256,1024]{0,1:T(8,128)(4,1)S(1)} %iota_compare_fusion), kind=kOutput, calls=%fused_computation.77 | convolution fusion | flops 1116209152 | bytes 35979264 | tf_op jit(solution)/shard_map/bkgqs,bskd->bqkgd/dot_general | solution.py:39
  279.1 2.3 pad_maximum_fusion
  281.4 15.3 %fusion.21 = (f32[1024]{0:T(1024)S(1)}, bf16[1,1024,2048]{2,1,0:T(8,128)(2,1)}) fusion(bf16[1024,2048]{0,1:T(8,128)(2,1)} %bitcast.234, bf16[2048,2048]{1,0:T(8,128)(2,1)} %all-gather.14.cloned.1.call-done, bf16[1,1024,2048]{2,1,0:T(8,128)(2,1)} %param.12), kind=kOutput, calls=%fused_computation.37 | convolution fusion | flops 8606710784 | bytes 20975616 | tf_op jit(solution)/shard_map/dot_general | solution.py:59
  296.7 3.0 all-gather.16.cloned.1.call-done
  299.7 42.3 %fusion.62 = bf16[1024,8192]{1,0:T(8,128)(2,1)} fusion(bf16[2048,8192]{1,0:T(8,128)(2,1)} %all-gather.16.cloned.1.call-done, bf16[1,1024,2048]{2,1,0:T(8,128)(2,1)} %get-tuple-element.18, f32[2048]{0:T(1024)S(1)} %copy-done.4, f32[1024]{0:T(1024)S(1)} %add_rsqrt_fusion), kind=kOutput, calls=%fused_computation.81 | convolution fusion | flops 34368126976 | bytes 54538240 | tf_op jit(solution)/shard_map/dot_general | solution.py:62
  342.0 67.1 %all-gather.18.cloned.1.call-done = bf16[2048,8192]{1,0:T(8,128)(2,1)} async-done(((bf16[64,8192]{1,0:T(8,128)(2,1)}), bf16[2048,8192]{1,0:T(8,128)(2,1)}) %all-gather.18.cloned.1.call-update) | async-done | bytes 33554448 | tf_op jit(solution)/shard_map/all_gather | solution.py:79
  409.1 42.2 %fusion.60 = bf16[1024,8192]{1,0:T(8,128)(2,1)} fusion(bf16[2048,8192]{1,0:T(8,128)(2,1)} %all-gather.18.cloned.1.call-done, bf16[1,1024,2048]{2,1,0:T(8,128)(2,1)} %get-tuple-element.18, f32[2048]{0:T(1024)S(1)} %copy-done.4, f32[1024]{0:T(1024)S(1)} %add_rsqrt_fusion), kind=kOutput, calls=%fused_computation.80 | convolution fusion | flops 34368126976 | bytes 54538240 | tf_op jit(solution)/shard_map/dot_general | solution.py:63
  451.3 67.4 %all-gather.20.cloned.1.call-done = bf16[8192,2048]{1,0:T(8,128)(2,1)} async-done(((bf16[256,2048]{1,0:T(8,128)(2,1)}), bf16[8192,2048]{1,0:T(8,128)(2,1)}) %all-gather.20.cloned.1.call-update) | async-done | bytes 33554448 | tf_op jit(solution)/shard_map/all_gather | solution.py:79
  518.7 47.7 %fusion.24 = bf16[1,1024,2048]{2,1,0:T(8,128)(2,1)} fusion(bf16[1,1024,2048]{2,1,0:T(8,128)(2,1)} %get-tuple-element.18, bf16[8192,2048]{1,0:T(8,128)(2,1)} %all-gather.20.cloned.1.call-done, bf16[1024,8192]{1,0:T(8,128)(2,1)} %fusion.60, bf16[1024,8192]{1,0:T(8,128)(2,1)} %fusion.62), kind=kOutput, calls=%fused_computation.40 | convolution fusion | flops 34437332992 | bytes 75497472 | tf_op jit(solution)/shard_map/dot_general | solution.py:65
  (44 shorter events, 0.5 us)
Async XLA Ops:
  7.2 61.2 %all-gather.10.cloned.1.call-start = ((), (), s32[]{:S(2)}) async-start(), calls=%async_computation.1 | async-start | bytes 2162688 | tf_op jit(solution)/shard_map/all_gather | solution.py:79
  8.0 84.5 %all-gather.8.cloned.1.call-start = ((), (), s32[]{:S(2)}) async-start(), calls=%async_computation | async-start | bytes 2162688 | tf_op jit(solution)/shard_map/all_gather | solution.py:79
  8.8 132.4 %all-gather.12.cloned.1.call-start = ((), (), s32[]{:S(2)}) async-start(), calls=%async_computation.2 | async-start | bytes 8650752 | tf_op jit(solution)/shard_map/all_gather | solution.py:79
  9.6 271.8 %all-gather.14.cloned.1.call-start = ((), (), s32[]{:S(2)}) async-start(), calls=%async_computation.3 | async-start | bytes 8650752 | tf_op jit(solution)/shard_map/all_gather | solution.py:79
  10.2 289.5 %all-gather.16.cloned.1.call-start = ((), (), s32[]{:S(2)}) async-start(), calls=%async_computation.4 | async-start | bytes 34603008 | tf_op jit(solution)/shard_map/all_gather | solution.py:79
  10.9 398.3 %all-gather.18.cloned.1.call-start = ((), (), s32[]{:S(2)}) async-start(), calls=%async_computation.5 | async-start | bytes 34603008 | tf_op jit(solution)/shard_map/all_gather | solution.py:79
  11.5 507.2 %all-gather.20.cloned.1.call-start = ((), (), s32[]{:S(2)}) async-start(), calls=%async_computation.6 | async-start | bytes 34603008 | tf_op jit(solution)/shard_map/all_gather | solution.py:79
  68.3 5.7 copy-start.2
  68.3 5.7 copy-start.3
  97.9 167.1 %copy-start.5 = (bf16[1024,512]{0,1:T(8,128)(2,1)}, bf16[1024,512]{0,1:T(8,128)(2,1)S(1)}, u32[]{:S(2)}) copy-start(bf16[1024,512]{0,1:T(8,128)(2,1)S(1)} %convolution_convert_fusion.1) | copy-start | bytes 3145732
  171.6 3.2 copy-start
  216.9 20.3 %slice-start = ((s8[33554432]{0:T(1024)(128)(4,1)}), s8[4194304]{0:T(1024)(128)(4,1)S(1)}, s32[]{:S(2)}) async-start(s8[33554432]{0:T(1024)(128)(4,1)} %bitcast.221), calls=%async_computation.7 | async-start | bytes 8388608
  216.9 20.3 %slice-start.1 = ((s8[33554432]{0:T(1024)(128)(4,1)}), s8[4194304]{0:T(1024)(128)(4,1)S(1)}, s32[]{:S(2)}) async-start(s8[33554432]{0:T(1024)(128)(4,1)} %bitcast.221), calls=%async_computation.8 | async-start | bytes 8388608
  216.9 20.3 %slice-start.2 = ((s8[33554432]{0:T(1024)(128)(4,1)}), s8[4194304]{0:T(1024)(128)(4,1)S(1)}, s32[]{:S(2)}) async-start(s8[33554432]{0:T(1024)(128)(4,1)} %bitcast.221), calls=%async_computation.9 | async-start | bytes 8388608
  216.9 20.3 %slice-start.3 = ((s8[33554432]{0:T(1024)(128)(4,1)}), s8[4194304]{0:T(1024)(128)(4,1)S(1)}, s32[]{:S(2)}) async-start(s8[33554432]{0:T(1024)(128)(4,1)} %bitcast.221), calls=%async_computation.10 | async-start | bytes 8388608
  216.9 20.3 %slice-start.4 = ((s8[33554432]{0:T(1024)(128)(4,1)}), s8[4194304]{0:T(1024)(128)(4,1)S(1)}, s32[]{:S(2)}) async-start(s8[33554432]{0:T(1024)(128)(4,1)} %bitcast.221), calls=%async_computation.11 | async-start | bytes 8388608
  223.6 13.6 %slice-start.5 = ((s8[33554432]{0:T(1024)(128)(4,1)}), s8[4194304]{0:T(1024)(128)(4,1)S(1)}, s32[]{:S(2)}) async-start(s8[33554432]{0:T(1024)(128)(4,1)} %bitcast.221), calls=%async_computation.12 | async-start | bytes 8388608
  223.6 13.6 %slice-start.6 = ((s8[33554432]{0:T(1024)(128)(4,1)}), s8[4194304]{0:T(1024)(128)(4,1)S(1)}, s32[]{:S(2)}) async-start(s8[33554432]{0:T(1024)(128)(4,1)} %bitcast.221), calls=%async_computation.13 | async-start | bytes 8388608
  223.6 14.2 %slice-start.7 = ((s8[33554432]{0:T(1024)(128)(4,1)}), s8[4194304]{0:T(1024)(128)(4,1)S(1)}, s32[]{:S(2)}) async-start(s8[33554432]{0:T(1024)(128)(4,1)} %bitcast.221), calls=%async_computation.14 | async-start | bytes 8388608
  265.0 14.1 %copy-start.1 = (bf16[1,256,8,4,64]{1,4,3,2,0:T(8,128)(2,1)S(1)}, bf16[1,256,8,4,64]{1,4,3,2,0:T(8,128)(2,1)}, u32[]{:S(2)}) copy-start(bf16[1,256,8,4,64]{1,4,3,2,0:T(8,128)(2,1)} %fusion.48) | copy-start | bytes 3145732
  281.4 18.3 %copy-start.4 = (f32[2048]{0:T(1024)S(1)}, f32[2048]{0:T(1024)}, u32[]{:S(2)}) copy-start(f32[2048]{0:T(1024)} %convert_element_type.205) | copy-start | bytes 24580
Sparse Core Ops, SparseCore 0:
  10.1 42.6 all-gather.9
  54.8 37.6 all-gather.7
  94.6 46.5 all-gather.11
  143.1 46.8 all-gather.13
  191.9 107.7 all-gather.15
  301.6 107.4 all-gather.17
  411.2 107.4 all-gather.19
where the time goes:
time: 583 us; the launch traced here: 574 us
  matrix products  246 us (42%)
  waiting for transfers between devices  202 us (35%)
  blocking collectives  50.1 us (9%)
  other arithmetic  45 us (8%)
  local copies, waits for them, and re-layouts  15.1 us (3%)
  between operations  14.9 us (3%)
    all_gather x1, waiting for transfers between devices, local_layer(): gather_rows(w_down)  67.4 us
    all_gather x1, waiting for transfers between devices, local_layer(): gather_rows(w_up)  67.1 us
    unnamed x1, blocking collectives  50.1 us
    dot_general x1, matrix products, decoder_layer(): jnp.dot(act_in, w_down, preferred_element_type=jnp.float32)  47.7 us
    all_gather x1, waiting for transfers between devices, local_layer(): gather_rows(w_query)  43.3 us
    dot_general x1, matrix products, decoder_layer(): jnp.dot(normed_mlp, w_gate, preferred_element_type=jnp.float32)  42.3 us
    dot_general x1, matrix products, decoder_layer(): jnp.dot(normed_mlp, w_up, preferred_element_type=jnp.float32)  42.2 us
    dot_general x4, matrix products, causal_attention(): jnp.einsum('bkgqs,bskd->bqkgd', prob_bf16, value_heads[:, :blk_stop], pre...  40.5 us
  transfers between devices with their start and end apart: 7, of which 5 were waited for; matrix products, arithmetic and copies ran while one was open for 44% of the time, Pallas kernels for 0%

commit v1 on v0

v1 whole, which is shorter than its diff:
```python
import functools
import math
import jax
import jax.numpy as jnp
from jax import lax
from jax.experimental import pallas as pl
from jax.experimental.pallas import tpu as pltpu
from jax.sharding import PartitionSpec as P

NORM_EPS = 1e-5
MESH = pl.DeviceIdType.MESH
LAG = 1
SLOTS = 2 * LAG + 2
READY = 4 * LAG + 1
ATTN_TICKS = (1, 2, 4, 4)
ROW_BLOCK = 256
BF16 = jnp.bfloat16
F32 = jnp.float32


def layer_kernel(cfg, x_hbm, gain_hbm, wq, wk, wv, wo, wg, wu, wd, cos_hbm, sin_hbm,
                 out_hbm, kt_hbm, vt_hbm, gath, gath_d, gath_g,
                 xv, hbuf, qbuf, rbuf, wbuf, wbuf_d, wl, wl_d, wl_g, gvm, gains, cosv, sinv,
                 send_sem, recv_sem, own_sem, load_sem, wsem, misc_sem, out_sem):
    side, seq, dim, ffn = cfg["side"], cfg["seq"], cfg["dim"], cfg["ffn"]
    width, half_w, width_d = cfg["width"], cfg["width"] // 2, cfg["width_d"]
    kv_dim = cfg["kv_dim"]
    n_q, n_o = cfg["q_dim"] // width, dim // width
    n_ffn, n_down = ffn // half_w, dim // width_d
    first_o = 1 + n_q
    first_f = first_o + n_o
    first_d = first_f + n_ffn
    n_piece = first_d + n_down
    rows, rows_d = cfg["rows"], cfg["rows_d"]
    rb = min(ROW_BLOCK, seq)

    me = lax.axis_index("fsdp")
    core = lax.rem(me, 2)
    px = lax.rem(me // 2, side)
    py = me // (2 * side)
    pa = px + core * (py - px)
    pb = py + core * (px - py)
    a_up, a_dn = lax.rem(pa + 1, side), lax.rem(pa + side - 1, side)
    b_up, b_dn = lax.rem(pb + 1, side), lax.rem(pb + side - 1, side)

    def device_at(a, b):
        y = b + core * (a - b)
        x = a + core * (b - a)
        return (y * side + x) * 2 + core

    dev_ap, dev_am = device_at(a_up, pb), device_at(a_dn, pb)
    dev_bp, dev_bm = device_at(pa, b_up), device_at(pa, b_dn)
    sibling = me + 1 - 2 * core

    def load(src, dst, sem):
        pltpu.make_async_copy(src, dst, sem).start()

    load(gain_hbm, wl_g, load_sem.at[n_piece])
    load(wk, wl.at[0, :, pl.ds(0, kv_dim)], load_sem.at[0])
    load(wv, wl.at[0, :, pl.ds(kv_dim, kv_dim)], load_sem.at[0])
    for c in range(n_q):
        load(wq.at[:, pl.ds(c * width, width)], wl.at[1 + c], load_sem.at[1 + c])
    load(x_hbm, xv, misc_sem.at[0])
    load(cos_hbm, cosv, misc_sem.at[1])
    load(sin_hbm, sinv, misc_sem.at[2])
    for c in range(n_o):
        load(wo.at[:, pl.ds(c * width, width)], wl.at[first_o + c], load_sem.at[first_o + c])

    def load_ffn(j, carry):
        col = pl.multiple_of(j * half_w, half_w)
        load(wg.at[:, pl.ds(col, half_w)], wl.at[first_f + j, :, pl.ds(0, half_w)], load_sem.at[first_f + j])
        load(wu.at[:, pl.ds(col, half_w)], wl.at[first_f + j, :, pl.ds(half_w, half_w)], load_sem.at[first_f + j])
        return carry

    lax.fori_loop(0, n_ffn, load_ffn, 0)

    def load_down(j, carry):
        col = pl.multiple_of(j * width_d, width_d)
        load(wd.at[:, pl.ds(col, width_d)], wl_d.at[j], load_sem.at[first_d + j])
        return carry

    lax.fori_loop(0, n_down, load_down, 0)

    dp = lax.axis_index("dp")
    barrier = pltpu.get_barrier_semaphore()
    for peer in (dev_ap, dev_am, dev_bp, dev_bm, sibling):
        pl.semaphore_signal(barrier, inc=1, device_id=(dp, peer), device_id_type=MESH)
    pl.semaphore_wait(barrier, 5)

    def remote(src, dst, stage, way, slot, peer):
        return pltpu.make_async_remote_copy(
            src_ref=src, dst_ref=dst, send_sem=send_sem.at[stage, way, slot], recv_sem=recv_sem.at[stage, way, slot],
            device_id=(dp, peer), device_id_type=MESH)

    def stage_op(stage, own, buf, n_rows, slot, wait_own):
        h = n_rows // 2
        mine = buf.at[core, pb, pa]

        def s1():
            return (remote(own, mine, 0, 0, slot, dev_ap), remote(own, mine, 0, 1, slot, dev_am))

        def s1_in():
            lo, hi = buf.at[core, pb, a_dn], buf.at[core, pb, a_up]
            return (remote(lo, lo, 0, 0, slot, dev_ap), remote(hi, hi, 0, 1, slot, dev_am))

        def s2():
            lo, hi = buf.at[core, pb, a_dn, pl.ds(0, h)], buf.at[core, pb, a_up, pl.ds(h, h)]
            return (remote(lo, lo, 1, 0, slot, dev_ap), remote(hi, hi, 1, 1, slot, dev_am))

        def s2_in():
            far = lax.rem(pa + 2, side)
            lo, hi = buf.at[core, pb, far, pl.ds(0, h)], buf.at[core, pb, far, pl.ds(h, h)]
            return (remote(lo, lo, 1, 0, slot, dev_ap), remote(hi, hi, 1, 1, slot, dev_am))

        def s3():
            line = buf.at[core, pb]
            return (remote(line, line, 2, 0, slot, dev_bp), remote(line, line, 2, 1, slot, dev_bm))

        def s3_in():
            lo, hi = buf.at[core, b_dn], buf.at[core, b_up]
            return (remote(lo, lo, 2, 0, slot, dev_bp), remote(hi, hi, 2, 1, slot, dev_bm))

        def s4():
            lo, hi = buf.at[core, b_dn, pl.ds(0, side // 2)], buf.at[core, b_up, pl.ds(side // 2, side // 2)]
            return (remote(lo, lo, 3, 0, slot, dev_bp), remote(hi, hi, 3, 1, slot, dev_bm))

        def s4_in():
            far = lax.rem(pb + 2, side)
            lo, hi = buf.at[core, far, pl.ds(0, side // 2)], buf.at[core, far, pl.ds(side // 2, side // 2)]
            return (remote(lo, lo, 3, 0, slot, dev_bp), remote(hi, hi, 3, 1, slot, dev_bm))

        def s5():
            plane = buf.at[core]
            return (remote(plane, plane, 4, 0, slot, sibling),)

        def s5_in():
            plane = buf.at[1 - core]
            return (remote(plane, plane, 4, 0, slot, sibling),)

        outs = (s1, s2, s3, s4, s5)
        ins = (s1_in, s2_in, s3_in, s4_in, s5_in)

        def keep():
            return pltpu.make_async_copy(own, mine, own_sem.at[slot])

        if stage == 0:
            wait_own()
            keep().start()
        else:
            for d in outs[stage - 1]():
                d.wait_send()
            for d in ins[stage - 1]():
                d.wait_recv()
            if stage == 2:
                keep().wait()
        if stage < 5:
            for d in outs[stage]():
                d.start()

    def run_stage(stage, p):
        slot = lax.rem(p, SLOTS)

        @pl.when(p == 0)
        def _():
            stage_op(stage, wl_g, gath_g, wl_g.shape[0], SLOTS,
                     lambda: pltpu.make_async_copy(wl_g, wl_g, load_sem.at[n_piece]).wait())

        @pl.when(jnp.logical_and(p >= 0, p < first_d))
        def _():
            own = wl.at[p]
            stage_op(stage, own, gath.at[p], rows, slot,
                     lambda: pltpu.make_async_copy(own, own, load_sem.at[p]).wait())

        @pl.when(jnp.logical_and(p >= first_d, p < n_piece))
        def _():
            own = wl_d.at[p - first_d]
            stage_op(stage, own, gath_d.at[p - first_d], rows_d, slot,
                     lambda: pltpu.make_async_copy(own, own, load_sem.at[p]).wait())

    def tick(t):
        for stage in range(5):
            run_stage(stage, t - stage * LAG)
        run_stage(5, t - READY)

    def fetch(buf, dst, sem):
        cps = [pltpu.make_async_copy(buf.at[0], dst.at[:, :, 0], sem)]
        for y in range(side):
            cps.append(pltpu.make_async_copy(buf.at[1, :, y], dst.at[y, :, 1], sem))
        for cp in cps:
            cp.start()

    def fetch_piece(p):
        slot = lax.rem(p, 2)
        fetch(gath.at[p], wbuf.at[slot], wsem.at[slot])

    def wait_piece(p):
        slot = lax.rem(p, 2)
        pltpu.make_async_copy(wbuf.at[slot], wbuf.at[slot], wsem.at[slot]).wait()
        return slot

    def fetch_down(i):
        slot = lax.rem(i, 2)
        fetch(gath_d.at[i], wbuf_d.at[slot], wsem.at[2 + slot])

    def wait_down(i):
        slot = lax.rem(i, 2)
        pltpu.make_async_copy(wbuf_d.at[slot], wbuf_d.at[slot], wsem.at[2 + slot]).wait()
        return slot

    def row_loop(body, block=rb):
        def step(i, carry):
            body(pl.ds(pl.multiple_of(i * block, block), block))
            return carry

        lax.fori_loop(0, seq // block, step, 0)

    def norm_rows(src, dst, gain_row):
        nb = min(64, seq)

        def body(rs):
            xx = src[rs, :].astype(F32)
            scale = lax.rsqrt(jnp.mean(xx * xx, axis=-1, keepdims=True) + NORM_EPS)
            dst[rs, :] = ((xx * scale) * gains[pl.ds(gain_row, 1), :]).astype(BF16)

        row_loop(body, nb)

    def weight(slot):
        return wbuf[slot].reshape(dim, width)

    lane = lax.broadcasted_iota(jnp.int32, (rb, 128), 1)
    low_half = lax.rem(lane, cfg["head"]) < cfg["head"] // 2

    def rope(block, rs):
        up = block.astype(BF16).astype(F32)
        swapped = jnp.where(low_half, pltpu.roll(up, 128 - cfg["head"] // 2, 1), pltpu.roll(up, cfg["head"] // 2, 1))
        return up * cosv[rs, :] + swapped * sinv[rs, :]

    n_kv = kv_dim // cfg["head"]
    head = cfg["head"]
    col_v = (0, n_kv * 128)
    col_k = (2 * n_kv * 128, 2 * n_kv * 128 + seq)
    col_t = 2 * n_kv * 128 + 2 * seq

    def pre(t, carry):
        tick(t)
        return carry

    lax.fori_loop(0, READY + 1, pre, 0)
    fetch_piece(0)
    pltpu.sync_copy(gath_g, gvm)
    pltpu.make_async_copy(x_hbm, xv, misc_sem.at[0]).wait()
    pltpu.make_async_copy(cos_hbm, cosv, misc_sem.at[1]).wait()
    pltpu.make_async_copy(sin_hbm, sinv, misc_sem.at[2]).wait()
    lane8 = lax.broadcasted_iota(jnp.int32, (8, 128), 1)
    for y in range(side):
        for x in range(side):
            for which in range(2):
                even = gvm[0, y, x, 8 * which:8 * which + 8, :]
                odd = gvm[1, x, y, 8 * which:8 * which + 8, :]
                c = (y * side + x) * 128
                gains[8 * which:8 * which + 8, c:c + 128] = jnp.where(lane8 < 64, even, odd)
    norm_rows(xv, hbuf, 0)

    tick(READY + 1)
    fetch_piece(1)
    slot = wait_piece(0)

    def kv_block(rs):
        acc = jnp.dot(hbuf[rs, :], weight(slot), preferred_element_type=F32)
        first = lane < head
        for c in range(kv_dim // 128):
            kr = rope(acc[:, c * 128:(c + 1) * 128], rs)
            kt = jnp.transpose(kr).astype(BF16)
            rbuf[c * 128:(c + 1) * 128, pl.ds(col_t + rs.start, rs.size)] = kt
            zero = jnp.zeros((head, rs.size), BF16)
            for g in range(2):
                kk = kt[g * head:(g + 1) * head]
                r0 = (2 * c + g) * 128
                rbuf[r0:r0 + head, pl.ds(col_k[0] + rs.start, rs.size)] = kk
                rbuf[r0 + head:r0 + 128, pl.ds(col_k[0] + rs.start, rs.size)] = zero
                rbuf[r0:r0 + head, pl.ds(col_k[1] + rs.start, rs.size)] = zero
                rbuf[r0 + head:r0 + 128, pl.ds(col_k[1] + rs.start, rs.size)] = kk
            vv = acc[:, kv_dim + c * 128:kv_dim + (c + 1) * 128]
            vt = jnp.transpose(vv).astype(BF16)
            rbuf[kv_dim + c * 128:kv_dim + (c + 1) * 128, pl.ds(col_t + rs.start, rs.size)] = vt
            turned = pltpu.roll(vv, head, 1)
            g0, g1 = 2 * c, 2 * c + 1
            rbuf[rs, col_v[0] + g0 * 128:col_v[0] + g0 * 128 + 128] = jnp.where(first, vv, 0.0).astype(BF16)
            rbuf[rs, col_v[1] + g0 * 128:col_v[1] + g0 * 128 + 128] = jnp.where(first, 0.0, turned).astype(BF16)
            rbuf[rs, col_v[0] + g1 * 128:col_v[0] + g1 * 128 + 128] = jnp.where(first, turned, 0.0).astype(BF16)
            rbuf[rs, col_v[1] + g1 * 128:col_v[1] + g1 * 128 + 128] = jnp.where(first, 0.0, vv).astype(BF16)

    row_loop(kv_block)
    kt_out = pltpu.make_async_copy(rbuf.at[pl.ds(0, kv_dim), pl.ds(col_t, seq)], kt_hbm, out_sem.at[n_down])
    vt_out = pltpu.make_async_copy(rbuf.at[pl.ds(kv_dim, kv_dim), pl.ds(col_t, seq)], vt_hbm, out_sem.at[n_down + 1])
    kt_out.start()
    vt_out.start()

    def q_step(c, carry):
        tick(READY + 2 + c)
        fetch_piece(2 + c)
        slot = wait_piece(1 + c)

        def q_block(rs):
            acc = jnp.dot(hbuf[rs, :], weight(slot), preferred_element_type=F32)
            for k in range(width // 128):
                dst = pl.ds(pl.multiple_of(c * width + k * 128, 128), 128)
                qbuf[rs, dst] = rope(acc[:, k * 128:(k + 1) * 128], rs).astype(BF16)

        row_loop(q_block)
        return carry

    lax.fori_loop(0, n_q, q_step, 0)
    t_now = READY + 2 + n_q

    n_pair = cfg["q_dim"] // 128
    pairs_per_kv = n_pair // n_kv
    qb = seq // len(ATTN_TICKS)
    scale = math.log2(math.e) * head ** -0.5
    causal = lax.broadcasted_iota(jnp.int32, (qb, qb), 0) >= lax.broadcasted_iota(jnp.int32, (qb, qb), 1)
    for i, n_t in enumerate(ATTN_TICKS):
        past = i * qb
        per = n_pair // n_t

        def one_pair(pi, i=i, past=past):
            g = pi // pairs_per_kv
            cs = pl.ds(pl.multiple_of(pi * 128, 128), 128)
            qp = qbuf[i * qb:(i + 1) * qb, cs]
            krow = pl.ds(pl.multiple_of(g * 128, 128), 128)
            total = None
            for hf in range(2):
                s_d = jnp.dot(qp, rbuf[krow, col_k[hf] + past:col_k[hf] + past + qb], preferred_element_type=F32)
                s_d = jnp.where(causal, s_d, -jnp.inf)
                m = jnp.max(s_d, axis=-1, keepdims=True)
                if past:
                    s_p = jnp.dot(qp, rbuf[krow, col_k[hf]:col_k[hf] + past], preferred_element_type=F32)
                    m = jnp.maximum(m, jnp.max(s_p, axis=-1, keepdims=True))
                e_d = jnp.exp2((s_d - m) * scale)
                den = jnp.sum(e_d, axis=-1, keepdims=True)
                if past:
                    e_p = jnp.exp2((s_p - m) * scale)
                    den = den + jnp.sum(e_p, axis=-1, keepdims=True)
                inv = 1.0 / den
                vcol = pl.ds(pl.multiple_of(col_v[hf] + g * 128, 128), 128)
                o = jnp.dot((e_d * inv).astype(BF16), rbuf[past:past + qb, vcol], preferred_element_type=F32)
                if past:
                    o = o + jnp.dot((e_p * inv).astype(BF16), rbuf[0:past, vcol], preferred_element_type=F32)
                total = o if total is None else total + o
            hbuf[i * qb:(i + 1) * qb, cs] = total.astype(BF16)

        def att_step(k, carry, one_pair=one_pair, per=per, base=t_now):
            tick(base + k)

            def inner(j, c2):
                one_pair(k * per + j)
                return c2

            lax.fori_loop(0, per, inner, 0)
            return carry

        lax.fori_loop(0, n_t, att_step, 0)
        t_now += n_t

    def o_step(c, carry):
        tick(t_now + c)
        fetch_piece(first_o + 1 + c)
        slot = wait_piece(first_o + c)

        def o_block(rs):
            acc = jnp.dot(hbuf[rs, :], weight(slot), preferred_element_type=F32)
            cs = pl.ds(pl.multiple_of(c * width, width), width)
            xv[rs, cs] = (xv[rs, cs].astype(F32) + acc.astype(BF16).astype(F32)).astype(BF16)

        row_loop(o_block)
        return carry

    lax.fori_loop(0, n_o, o_step, 0)
    t_now += n_o
    kt_out.wait()
    vt_out.wait()
    norm_rows(xv, qbuf, 8)

    def f_step(j, carry):
        @pl.when(lax.rem(j, 2) == 0)
        def _():
            tick(t_now + j // 2)

        @pl.when(j + 1 < n_ffn)
        def _():
            fetch_piece(first_f + j + 1)

        @pl.when(j + 1 == n_ffn)
        def _():
            fetch_down(0)

        slot = wait_piece(first_f + j)

        def f_block(rs):
            acc = jnp.dot(qbuf[rs, :], weight(slot), preferred_element_type=F32)
            gate = acc[:, :half_w].astype(BF16).astype(F32)
            up = acc[:, half_w:].astype(BF16).astype(F32)
            cs = pl.ds(pl.multiple_of(j * half_w, half_w), half_w)
            rbuf[rs, cs] = (jax.nn.silu(gate) * up).astype(BF16)

        row_loop(f_block)
        return carry

    lax.fori_loop(0, n_ffn, f_step, 0)
    t_now += (n_ffn + 1) // 2

    t_left = n_piece + READY - t_now
    skip = n_down - 1 - t_left

    def out_copy(i):
        cs = pl.ds(pl.multiple_of(i * width_d, width_d), width_d)
        return pltpu.make_async_copy(xv.at[:, cs], out_hbm.at[:, cs], out_sem.at[i])

    def d_step(i, carry):
        @pl.when(jnp.logical_and(i >= skip, i < n_down - 1))
        def _():
            tick(t_now + i - skip)

        @pl.when(i + 1 < n_down)
        def _():
            fetch_down(i + 1)

        slot = wait_down(i)
        cs = pl.ds(pl.multiple_of(i * width_d, width_d), width_d)

        def d_block(rs):
            acc = jnp.dot(rbuf[rs, :], wbuf_d[slot].reshape(ffn, width_d), preferred_element_type=F32)
            xv[rs, cs] = (xv[rs, cs].astype(F32) + acc.astype(BF16).astype(F32)).astype(BF16)

        row_loop(d_block)
        out_copy(i).start()
        return carry

    lax.fori_loop(0, n_down, d_step, 0)

    def finish(i, carry):
        out_copy(i).wait()
        return carry

    lax.fori_loop(0, n_down, finish, 0)
    assert skip >= 0 and sum(ATTN_TICKS) - skip <= n_down


def solution(mesh, width=1024, width_d=256):
    n_dev = mesh.shape["fsdp"]
    side = math.isqrt(n_dev // 2)
    tok_spec = P(("dp", "fsdp"), None, None)
    cache_spec = P(("dp", "fsdp"), None, None, None)
    row_spec = P("fsdp", None)
    gain_spec = P("fsdp")
    table_spec = P(None, None)

    def local_layer(hidden, g_attn, w_query, w_key, w_value, w_out, g_mlp, w_gate, w_up, w_down, cos_tab, sin_tab):
        _, seq, dim = hidden.shape
        rows, q_dim = w_query.shape
        kv_dim = w_key.shape[1]
        ffn = w_gate.shape[1]
        rows_d = w_down.shape[0]
        head = 2 * cos_tab.shape[1]
        cfg = dict(side=side, seq=seq, dim=dim, ffn=ffn, width=width, width_d=width_d, kv_dim=kv_dim, q_dim=q_dim,
                   rows=rows, rows_d=rows_d, head=head)
        assert 2 * kv_dim == width and rows == 64 and rows * n_dev == dim
        gain_tile = jnp.concatenate([
            jnp.broadcast_to(jnp.tile(g_attn.astype(F32), 2)[None, :], (8, 128)),
            jnp.broadcast_to(jnp.tile(g_mlp.astype(F32), 2)[None, :], (8, 128))], axis=0)
        cos4 = jnp.concatenate([cos_tab] * 4, axis=1)
        sin4 = jnp.concatenate([-sin_tab, sin_tab] * 2, axis=1)
        n_wide = (2 * kv_dim + q_dim + dim + 2 * ffn) // width
        n_down = dim // width_d
        n_piece = n_wide + n_down
        hbm = pl.BlockSpec(memory_space=pl.ANY)
        res = pl.pallas_call(
            functools.partial(layer_kernel, cfg),
            out_shape=(
                jax.ShapeDtypeStruct((seq, dim), BF16),
                jax.ShapeDtypeStruct((kv_dim, seq), BF16),
                jax.ShapeDtypeStruct((kv_dim, seq), BF16),
                jax.ShapeDtypeStruct((n_wide, 2, side, side, rows, width), BF16),
                jax.ShapeDtypeStruct((n_down, 2, side, side, rows_d, width_d), BF16),
                jax.ShapeDtypeStruct((2, side, side, 16, 128), F32)),
            in_specs=[hbm] * 11,
            out_specs=[hbm] * 6,
            scratch_shapes=[
                pltpu.VMEM((seq, dim), BF16),
                pltpu.VMEM((seq, max(dim, q_dim)), BF16),
                pltpu.VMEM((seq, max(dim, q_dim)), BF16),
                pltpu.VMEM((max(seq, 2 * kv_dim), ffn), BF16),
                pltpu.VMEM((2, side, side, 2, rows, width), BF16),
                pltpu.VMEM((2, side, side, 2, rows_d, width_d), BF16),
                pltpu.VMEM((n_wide, rows, width), BF16),
                pltpu.VMEM((n_down, rows_d, width_d), BF16),
                pltpu.VMEM((16, 128), F32),
                pltpu.VMEM((2, side, side, 16, 128), F32),
                pltpu.VMEM((16, dim), F32),
                pltpu.VMEM((seq, 128), F32),
                pltpu.VMEM((seq, 128), F32),
                pltpu.SemaphoreType.DMA((5, 2, SLOTS + 1)),
                pltpu.SemaphoreType.DMA((5, 2, SLOTS + 1)),
                pltpu.SemaphoreType.DMA((SLOTS + 1,)),
                pltpu.SemaphoreType.DMA((n_piece + 1,)),
                pltpu.SemaphoreType.DMA((4,)),
                pltpu.SemaphoreType.DMA((3,)),
                pltpu.SemaphoreType.DMA((n_down + 2,)),
            ],
            compiler_params=pltpu.CompilerParams(
                collective_id=0, has_side_effects=True, vmem_limit_bytes=67043328),
        )(hidden[0], gain_tile, w_query, w_key, w_value, w_out, w_gate, w_up, w_down, cos4, sin4)
        out, kt, vt = res[:3]

        def cache(t):
            return jnp.transpose(t.reshape(1, kv_dim // head, head, seq), (0, 3, 1, 2))

        return out[None], cache(kt), cache(vt)

    return jax.shard_map(local_layer, mesh=mesh, in_specs=(tok_spec, gain_spec, row_spec, row_spec, row_spec, row_spec, gain_spec, row_spec, row_spec, row_spec, table_spec, table_spec), out_specs=(tok_spec, cache_spec, cache_spec), check_vma=False)
```

time: 583 us -> 382 us (0.66); the launches traced: 574 us -> 382 us
  Pallas kernels: 0 us -> 367 us
  matrix products: 246 us -> 0 us
  waiting for transfers between devices: 202 us -> 0 us
  blocking collectives: 50.1 us -> 0 us
  other arithmetic: 45 us -> 3.37 us
  between operations: 14.9 us -> 0.69 us
    pallas_call x0 -> x1, Pallas kernels: none -> 367 us  [local_layer(): pl.pallas_call(functools.partial(layer_kernel, cfg), out_shape=(jax.Shape...]
    dot_general x15 -> x0, matrix products: 246 us -> none  [the longest x1 47.7 us: decoder_layer(): jnp.dot(act_in, w_down, preferred_element_type=jnp.float32)]
    all_gather x7 -> x0, waiting for transfers between devices: 198 us -> none  [the longest x1 67.4 us: local_layer(): gather_rows(w_down)]
    unnamed x1 -> x0, blocking collectives: 50.1 us -> none
    reduce_sum x5 -> x0, other arithmetic: 35.1 us -> none  [the longest x4 32 us: causal_attention(): prob_bf16 = jax.nn.softmax(scores, axis=-1).astype(jnp.bfloat16)]
    convert_element_type x1 -> x0, local copies, waits for them, and re-layouts: 9.5 us -> none  [apply_rope(): upcast = heads_in.astype(jnp.float32)]
  transfers between devices with their start and end apart: 7 -> 0, of which waited for: 5 -> 0; matrix products, arithmetic and copies ran while one was open for 44% -> 0% of each run, Pallas kernels for 0% -> 0%
where the time goes in v1:
time: 382 us
  Pallas kernels  367 us (96%)
  local copies, waits for them, and re-layouts  10.8 us (3%)
    pallas_call x1, Pallas kernels, local_layer(): pl.pallas_call(functools.partial(layer_kernel, cfg), out_shape=(jax.Shape...  367 us
    unnamed x9, local copies, waits for them, and re-layouts  9.09 us

profile of v1, /device:TPU:97, one launch (start us, length us, event | category | flops | bytes accessed | tf_op | source)
XLA Modules:
  0.0 382.1 jit_solution(10811114805917834189)
XLA Ops:
  0.6 0.7 tile.4
  1.3 0.1 broadcast_in_dim.17
  1.4 0.7 tile.5
  2.0 0.1 broadcast_in_dim.19
  2.1 0.6 pad_maximum_fusion.2.gain_hbm
  2.7 0.9 neg.3
  3.6 0.2 copy.26
  3.8 1.1 copy.22
  5.0 1.1 copy.27
  6.1 1.9 pad_maximum_fusion
  7.9 367.3 %shard_map.139 = (bf16[1024,2048]{1,0:T(8,128)(2,1)}, bf16[512,1024]{1,0:T(8,128)(2,1)}, bf16[512,1024]{1,0:T(8,128)(2,1)}, bf16[21,2,4,4,64,1024]{5,4,3,2,1,0:T...) custom-call(bf16[1024,2048]{1,0:T(8,128)(2,1)} %bitcast.8, ...), custom_call_target="tpu_custom_call" | custom-call | tf_op jit(solution)/shard_map/pallas_call | solution.py:476
  375.2 0.0 copy-start.1
  375.3 0.0 copy-start
  375.3 4.9 %copy.33 = bf16[1,1024,2048]{2,1,0:T(8,128)(2,1)} copy(bf16[1,1024,2048]{2,1,0:T(8,128)(2,1)} %bitcast.9) | data formatting | bytes 8388608
  380.2 0.0 copy-done.1
  380.2 1.0 copy.34
  381.2 0.0 copy-done
  381.2 1.0 copy.35
  (2 shorter events, 0.0 us)
Async XLA Ops:
  375.2 5.0 %copy-start.1 = (bf16[512,1024]{1,0:T(8,128)(2,1)S(1)}, bf16[512,1024]{1,0:T(8,128)(2,1)}, u32[]{:S(2)}) copy-start(bf16[512,1024]{1,0:T(8,128)(2,1)} %get-tuple-element.7) | copy-start | bytes 3145732
  375.3 5.9 %copy-start = (bf16[512,1024]{1,0:T(8,128)(2,1)S(1)}, bf16[512,1024]{1,0:T(8,128)(2,1)}, u32[]{:S(2)}) copy-start(bf16[512,1024]{1,0:T(8,128)(2,1)} %get-tuple-element.8) | copy-start | bytes 3145732

commit v2 on v1

--- a/solution.py
+++ b/solution.py
@@ -9,8 +9,8 @@
 
 NORM_EPS = 1e-5
 MESH = pl.DeviceIdType.MESH
-LAG = 1
-SLOTS = 2 * LAG + 2
+LAG = 2
+SLOTS = 2 * LAG + 4
 READY = 4 * LAG + 1
 ATTN_TICKS = (1, 2, 4, 4)
 ROW_BLOCK = 256
@@ -20,7 +20,7 @@
 
 def layer_kernel(cfg, x_hbm, gain_hbm, wq, wk, wv, wo, wg, wu, wd, cos_hbm, sin_hbm,
                  out_hbm, kt_hbm, vt_hbm, gath, gath_d, gath_g,
-                 xv, hbuf, qbuf, rbuf, wbuf, wbuf_d, wl, wl_d, wl_g, gvm, gains, cosv, sinv,
+                 xv, hbuf, qbuf, rbuf, wbuf, wbuf_d, wl, wl_d, wl_g, gvm, gains, cosv, sinv, cost, sint,
                  send_sem, recv_sem, own_sem, load_sem, wsem, misc_sem, out_sem):
     side, seq, dim, ffn = cfg["side"], cfg["seq"], cfg["dim"], cfg["ffn"]
     width, half_w, width_d = cfg["width"], cfg["width"] // 2, cfg["width_d"]
@@ -33,6 +33,7 @@
     n_piece = first_d + n_down
     rows, rows_d = cfg["rows"], cfg["rows_d"]
     rb = min(ROW_BLOCK, seq)
+    tb = min(128, seq)
 
     me = lax.axis_index("fsdp")
     core = lax.rem(me, 2)
@@ -61,8 +62,8 @@
     for c in range(n_q):
         load(wq.at[:, pl.ds(c * width, width)], wl.at[1 + c], load_sem.at[1 + c])
     load(x_hbm, xv, misc_sem.at[0])
-    load(cos_hbm, cosv, misc_sem.at[1])
-    load(sin_hbm, sinv, misc_sem.at[2])
+    load(cos_hbm, cost, misc_sem.at[1])
+    load(sin_hbm, sint, misc_sem.at[2])
     for c in range(n_o):
         load(wo.at[:, pl.ds(c * width, width)], wl.at[first_o + c], load_sem.at[first_o + c])
 
@@ -129,15 +130,27 @@
             lo, hi = buf.at[core, far, pl.ds(0, side // 2)], buf.at[core, far, pl.ds(side // 2, side // 2)]
             return (remote(lo, lo, 3, 0, slot, dev_bp), remote(hi, hi, 3, 1, slot, dev_bm))
 
+        def hand(line, row, way):
+            ref = buf.at[core, line]
+            return remote(ref, ref, row, way, slot, sibling)
+
+        def hand_in(line, row, way):
+            ref = buf.at[1 - core, line]
+            return remote(ref, ref, row, way, slot, sibling)
+
+        def s3_all():
+            return s3() + (hand(pb, 4, 0),)
+
+        def s4_all():
+            return s4() + (hand(b_dn, 4, 1), hand(b_up, 5, 0))
+
         def s5():
-            plane = buf.at[core]
-            return (remote(plane, plane, 4, 0, slot, sibling),)
+            return (hand(lax.rem(pb + 2, side), 5, 1),)
 
         def s5_in():
-            plane = buf.at[1 - core]
-            return (remote(plane, plane, 4, 0, slot, sibling),)
-
-        outs = (s1, s2, s3, s4, s5)
+            return (hand_in(pa, 4, 0), hand_in(a_dn, 4, 1), hand_in(a_up, 5, 0), hand_in(lax.rem(pa + 2, side), 5, 1))
+
+        outs = (s1, s2, s3_all, s4_all, s5)
         ins = (s1_in, s2_in, s3_in, s4_in, s5_in)
 
         def keep():
@@ -249,8 +262,13 @@
     fetch_piece(0)
     pltpu.sync_copy(gath_g, gvm)
     pltpu.make_async_copy(x_hbm, xv, misc_sem.at[0]).wait()
-    pltpu.make_async_copy(cos_hbm, cosv, misc_sem.at[1]).wait()
-    pltpu.make_async_copy(sin_hbm, sinv, misc_sem.at[2]).wait()
+    pltpu.make_async_copy(cos_hbm, cost, misc_sem.at[1]).wait()
+    pltpu.make_async_copy(sin_hbm, sint, misc_sem.at[2]).wait()
+    for k in range(seq // tb):
+        cc, ss = cost[:, k * tb:(k + 1) * tb], sint[:, k * tb:(k + 1) * tb]
+        cosv[k * tb:(k + 1) * tb, :] = jnp.transpose(jnp.concatenate([cc] * 4, axis=0))
+        sinv[k * tb:(k + 1) * tb, :] = jnp.transpose(jnp.concatenate([-ss, ss] * 2, axis=0))
+
     lane8 = lax.broadcasted_iota(jnp.int32, (8, 128), 1)
     for y in range(side):
         for x in range(side):
@@ -258,7 +276,7 @@
                 even = gvm[0, y, x, 8 * which:8 * which + 8, :]
                 odd = gvm[1, x, y, 8 * which:8 * which + 8, :]
                 c = (y * side + x) * 128
-                gains[8 * which:8 * which + 8, c:c + 128] = jnp.where(lane8 < 64, even, odd)
+                gains[8 * which:8 * which + 8, c:c + 128] = jnp.where(lane8 < 64, even, pltpu.roll(odd, 64, 1))
     norm_rows(xv, hbuf, 0)
 
     tick(READY + 1)
@@ -416,11 +434,7 @@
         return pltpu.make_async_copy(xv.at[:, cs], out_hbm.at[:, cs], out_sem.at[i])
 
     def d_step(i, carry):
-        @pl.when(jnp.logical_and(i >= skip, i < n_down - 1))
-        def _():
-            tick(t_now + i - skip)
-
-        @pl.when(i + 1 < n_down)
+        @pl.when(i < skip)
         def _():
             fetch_down(i + 1)
 
@@ -433,6 +447,12 @@
 
         row_loop(d_block)
         out_copy(i).start()
+
+        @pl.when(jnp.logical_and(i >= skip, i < n_down - 1))
+        def _():
+            tick(t_now + i - skip)
+            fetch_down(i + 1)
+
         return carry
 
     lax.fori_loop(0, n_down, d_step, 0)
@@ -443,6 +463,19 @@
 
     lax.fori_loop(0, n_down, finish, 0)
     assert skip >= 0 and sum(ATTN_TICKS) - skip <= n_down
+
+
+def copy_kernel(a, b, c, a_out, b_out, c_out):
+    a_out[...] = a[...]
+    b_out[...] = b[...]
+    c_out[...] = c[...]
+
+
+def fresh_copy(a, b, c, steps=4):
+    specs = [pl.BlockSpec((t.shape[0] // steps, t.shape[1]), lambda i: (i, 0)) for t in (a, b, c)]
+    return pl.pallas_call(
+        copy_kernel, grid=(steps,), in_specs=specs, out_specs=specs,
+        out_shape=[jax.ShapeDtypeStruct(t.shape, t.dtype) for t in (a, b, c)])(a, b, c)
 
 
 def solution(mesh, width=1024, width_d=256):
@@ -464,11 +497,8 @@
         cfg = dict(side=side, seq=seq, dim=dim, ffn=ffn, width=width, width_d=width_d, kv_dim=kv_dim, q_dim=q_dim,
                    rows=rows, rows_d=rows_d, head=head)
         assert 2 * kv_dim == width and rows == 64 and rows * n_dev == dim
-        gain_tile = jnp.concatenate([
-            jnp.broadcast_to(jnp.tile(g_attn.astype(F32), 2)[None, :], (8, 128)),
-            jnp.broadcast_to(jnp.tile(g_mlp.astype(F32), 2)[None, :], (8, 128))], axis=0)
-        cos4 = jnp.concatenate([cos_tab] * 4, axis=1)
-        sin4 = jnp.concatenate([-sin_tab, sin_tab] * 2, axis=1)
+        both = jnp.stack([g_attn, g_mlp]).astype(F32)
+        gain_tile = jnp.broadcast_to(jnp.pad(both, ((0, 0), (0, 128 - rows)))[:, None, :], (2, 8, 128)).reshape(16, 128)
         n_wide = (2 * kv_dim + q_dim + dim + 2 * ffn) // width
         n_down = dim // width_d
         n_piece = n_wide + n_down
@@ -498,8 +528,10 @@
                 pltpu.VMEM((16, dim), F32),
                 pltpu.VMEM((seq, 128), F32),
                 pltpu.VMEM((seq, 128), F32),
-                pltpu.SemaphoreType.DMA((5, 2, SLOTS + 1)),
-                pltpu.SemaphoreType.DMA((5, 2, SLOTS + 1)),
+                pltpu.VMEM((head // 2, seq), F32),
+                pltpu.VMEM((head // 2, seq), F32),
+                pltpu.SemaphoreType.DMA((6, 2, SLOTS + 1)),
+                pltpu.SemaphoreType.DMA((6, 2, SLOTS + 1)),
                 pltpu.SemaphoreType.DMA((SLOTS + 1,)),
                 pltpu.SemaphoreType.DMA((n_piece + 1,)),
                 pltpu.SemaphoreType.DMA((4,)),
@@ -508,8 +540,8 @@
             ],
             compiler_params=pltpu.CompilerParams(
                 collective_id=0, has_side_effects=True, vmem_limit_bytes=67043328),
-        )(hidden[0], gain_tile, w_query, w_key, w_value, w_out, w_gate, w_up, w_down, cos4, sin4)
-        out, kt, vt = res[:3]
+        )(hidden[0], gain_tile, w_query, w_key, w_value, w_out, w_gate, w_up, w_down, cos_tab.T, sin_tab.T)
+        out, kt, vt = fresh_copy(*res[:3])
 
         def cache(t):
             return jnp.transpose(t.reshape(1, kv_dim // head, head, seq), (0, 3, 1, 2))

time: 382 us -> 381 us (level)
  Pallas kernels: 367 us -> 379 us
  local copies, waits for them, and re-layouts: 10.8 us -> 0.6 us
    unnamed x9 -> x0, local copies, waits for them, and re-layouts: 9.09 us -> none
    pallas_call x1, Pallas kernels: 367 us -> 373 us  [local_layer(): pl.pallas_call(functools.partial(layer_kernel, cfg), out_shape=(jax.Shape...]
    pallas_call x0 -> x1, Pallas kernels: none -> 5.81 us  [fresh_copy(): pl.pallas_call(copy_kernel, grid=(steps,), in_specs=specs, out_specs=spec...]
where the time goes in v2:
time: 381 us
  Pallas kernels  379 us (99%)
    pallas_call x1, Pallas kernels, local_layer(): pl.pallas_call(functools.partial(layer_kernel, cfg), out_shape=(jax.Shape...  373 us

profile of v2, /device:TPU:97, one launch (start us, length us, event | category | flops | bytes accessed | tf_op | source)
XLA Modules:
  0.0 381.0 jit_solution(10478107698403988391)
XLA Ops:
  0.6 0.7 fusion.3
  1.3 0.6 broadcast_bitcast_fusion.gain_hbm
  1.9 373.2 %shard_map.139 = (bf16[1024,2048]{1,0:T(8,128)(2,1)}, bf16[512,1024]{1,0:T(8,128)(2,1)}, bf16[512,1024]{1,0:T(8,128)(2,1)}, bf16[21,2,4,4,64,1024]{5,4,3,2,1,0:T...) custom-call(bf16[1024,2048]{1,0:T(8,128)(2,1)} %bitcast.14, ...), custom_call_target="tpu_custom_call" | custom-call | tf_op jit(solution)/shard_map/pallas_call | solution.py:506
  375.1 5.8 %shard_map.140 = (bf16[1024,2048]{1,0:T(8,128)(2,1)}, bf16[512,1024]{1,0:T(8,128)(2,1)}, bf16[512,1024]{1,0:T(8,128)(2,1)}) custom-call(bf16[1024,2048]{1,0:T(8,128)(2,1)} %get-tuple-element.9.a, bf16[512,1024]{1,0:T(8,128)(2,1)} %get-tuple-element.10.b, bf16[512,1024]{1,0:T(8,128)(2,1)} %get-tuple-element.11.c), custom_call_target="tpu_custom_call" | custom-call | tf_op jit(solution)/shard_map/pallas_call | solution.py:476

commit v3 on v2

--- a/solution.py
+++ b/solution.py
@@ -12,7 +12,8 @@
 LAG = 2
 SLOTS = 2 * LAG + 4
 READY = 4 * LAG + 1
-ATTN_TICKS = (1, 2, 4, 4)
+ATTN_TICKS = (1, 1, 2, 2)
+FFN_PAIRED = 13
 ROW_BLOCK = 256
 BF16 = jnp.bfloat16
 F32 = jnp.float32
@@ -258,17 +259,17 @@
         tick(t)
         return carry
 
-    lax.fori_loop(0, READY + 1, pre, 0)
-    fetch_piece(0)
-    pltpu.sync_copy(gath_g, gvm)
-    pltpu.make_async_copy(x_hbm, xv, misc_sem.at[0]).wait()
+    lax.fori_loop(0, LAG + 1, pre, 0)
     pltpu.make_async_copy(cos_hbm, cost, misc_sem.at[1]).wait()
     pltpu.make_async_copy(sin_hbm, sint, misc_sem.at[2]).wait()
     for k in range(seq // tb):
         cc, ss = cost[:, k * tb:(k + 1) * tb], sint[:, k * tb:(k + 1) * tb]
         cosv[k * tb:(k + 1) * tb, :] = jnp.transpose(jnp.concatenate([cc] * 4, axis=0))
         sinv[k * tb:(k + 1) * tb, :] = jnp.transpose(jnp.concatenate([-ss, ss] * 2, axis=0))
-
+    lax.fori_loop(LAG + 1, READY + 1, pre, 0)
+    fetch_piece(0)
+    pltpu.sync_copy(gath_g, gvm)
+    pltpu.make_async_copy(x_hbm, xv, misc_sem.at[0]).wait()
     lane8 = lax.broadcasted_iota(jnp.int32, (8, 128), 1)
     for y in range(side):
         for x in range(side):
@@ -279,8 +280,6 @@
                 gains[8 * which:8 * which + 8, c:c + 128] = jnp.where(lane8 < 64, even, pltpu.roll(odd, 64, 1))
     norm_rows(xv, hbuf, 0)
 
-    tick(READY + 1)
-    fetch_piece(1)
     slot = wait_piece(0)
 
     def kv_block(rs):
@@ -315,8 +314,8 @@
     vt_out.start()
 
     def q_step(c, carry):
-        tick(READY + 2 + c)
-        fetch_piece(2 + c)
+        tick(READY + 1 + c)
+        fetch_piece(1 + c)
         slot = wait_piece(1 + c)
 
         def q_block(rs):
@@ -329,7 +328,7 @@
         return carry
 
     lax.fori_loop(0, n_q, q_step, 0)
-    t_now = READY + 2 + n_q
+    t_now = READY + 1 + n_q
 
     n_pair = cfg["q_dim"] // 128
     pairs_per_kv = n_pair // n_kv
@@ -378,6 +377,8 @@
 
         lax.fori_loop(0, n_t, att_step, 0)
         t_now += n_t
+        if i == 0:
+            fetch_piece(first_o)
 
     def o_step(c, carry):
         tick(t_now + c)
@@ -398,18 +399,28 @@
     vt_out.wait()
     norm_rows(xv, qbuf, 8)
 
+    ticks_by = [min(j, FFN_PAIRED) // 2 + (j < FFN_PAIRED) + max(0, j - FFN_PAIRED + 1) + (j >= FFN_PAIRED) * (FFN_PAIRED % 2)
+                for j in range(n_ffn)]
+    early = [t_now - 1 + ticks_by[j] - READY >= first_f + j + 1 and j + 1 < n_ffn for j in range(n_ffn)]
+    n_early = sum(early)
+    assert all(early[:n_early]) and all(t_now - 1 + ticks_by[j] - READY >= first_f + j for j in range(n_ffn))
+
     def f_step(j, carry):
-        @pl.when(lax.rem(j, 2) == 0)
+        @pl.when(jnp.logical_and(lax.rem(j, 2) == 0, j < FFN_PAIRED))
         def _():
             tick(t_now + j // 2)
 
-        @pl.when(j + 1 < n_ffn)
+        @pl.when(j >= FFN_PAIRED)
+        def _():
+            tick(t_now + (FFN_PAIRED + 1) // 2 + j - FFN_PAIRED)
+
+        @pl.when(j > n_early)
+        def _():
+            fetch_piece(first_f + j)
+
+        @pl.when(j < n_early)
         def _():
             fetch_piece(first_f + j + 1)
-
-        @pl.when(j + 1 == n_ffn)
-        def _():
-            fetch_down(0)
 
         slot = wait_piece(first_f + j)
 
@@ -424,20 +435,15 @@
         return carry
 
     lax.fori_loop(0, n_ffn, f_step, 0)
-    t_now += (n_ffn + 1) // 2
-
-    t_left = n_piece + READY - t_now
-    skip = n_down - 1 - t_left
+    t_now += ticks_by[-1]
 
     def out_copy(i):
         cs = pl.ds(pl.multiple_of(i * width_d, width_d), width_d)
         return pltpu.make_async_copy(xv.at[:, cs], out_hbm.at[:, cs], out_sem.at[i])
 
     def d_step(i, carry):
-        @pl.when(i < skip)
-        def _():
-            fetch_down(i + 1)
-
+        tick(t_now + i)
+        fetch_down(i)
         slot = wait_down(i)
         cs = pl.ds(pl.multiple_of(i * width_d, width_d), width_d)
 
@@ -447,12 +453,6 @@
 
         row_loop(d_block)
         out_copy(i).start()
-
-        @pl.when(jnp.logical_and(i >= skip, i < n_down - 1))
-        def _():
-            tick(t_now + i - skip)
-            fetch_down(i + 1)
-
         return carry
 
     lax.fori_loop(0, n_down, d_step, 0)
@@ -462,7 +462,7 @@
         return carry
 
     lax.fori_loop(0, n_down, finish, 0)
-    assert skip >= 0 and sum(ATTN_TICKS) - skip <= n_down
+    assert t_now + n_down >= n_piece + READY
 
 
 def copy_kernel(a, b, c, a_out, b_out, c_out):

time: 381 us -> 352 us (0.924)
  Pallas kernels: 379 us -> 350 us
    pallas_call x1, Pallas kernels: 373 us -> 344 us  [local_layer(): pl.pallas_call(functools.partial(layer_kernel, cfg), out_shape=(jax.Shape...]
where the time goes in v3:
time: 352 us; the launch traced here: 351 us
  Pallas kernels  350 us (99%)
    pallas_call x1, Pallas kernels, local_layer(): pl.pallas_call(functools.partial(layer_kernel, cfg), out_shape=(jax.Shape...  344 us

profile of v3, /device:TPU:97, one launch (start us, length us, event | category | flops | bytes accessed | tf_op | source)
XLA Modules:
  0.0 351.5 jit_solution(5998313436236110410)
XLA Ops:
  0.6 0.7 fusion.3
  1.3 0.6 broadcast_bitcast_fusion.gain_hbm
  1.9 343.8 %shard_map.139 = (bf16[1024,2048]{1,0:T(8,128)(2,1)}, bf16[512,1024]{1,0:T(8,128)(2,1)}, bf16[512,1024]{1,0:T(8,128)(2,1)}, bf16[21,2,4,4,64,1024]{5,4,3,2,1,0:T...) custom-call(bf16[1024,2048]{1,0:T(8,128)(2,1)} %bitcast.14, ...), custom_call_target="tpu_custom_call" | custom-call | tf_op jit(solution)/shard_map/pallas_call | solution.py:506
  345.7 5.8 %shard_map.140 = (bf16[1024,2048]{1,0:T(8,128)(2,1)}, bf16[512,1024]{1,0:T(8,128)(2,1)}, bf16[512,1024]{1,0:T(8,128)(2,1)}) custom-call(bf16[1024,2048]{1,0:T(8,128)(2,1)} %get-tuple-element.9.a, bf16[512,1024]{1,0:T(8,128)(2,1)} %get-tuple-element.10.b, bf16[512,1024]{1,0:T(8,128)(2,1)} %get-tuple-element.11.c), custom_call_target="tpu_custom_call" | custom-call | tf_op jit(solution)/shard_map/pallas_call | solution.py:476

commit v4 on v3

--- a/solution.py
+++ b/solution.py
@@ -15,14 +15,15 @@
 ATTN_TICKS = (1, 1, 2, 2)
 FFN_PAIRED = 13
 ROW_BLOCK = 256
+VMEM_MAIN = 38 << 20
 BF16 = jnp.bfloat16
 F32 = jnp.float32
 
 
 def layer_kernel(cfg, x_hbm, gain_hbm, wq, wk, wv, wo, wg, wu, wd, cos_hbm, sin_hbm,
-                 out_hbm, kt_hbm, vt_hbm, gath, gath_d, gath_g,
-                 xv, hbuf, qbuf, rbuf, wbuf, wbuf_d, wl, wl_d, wl_g, gvm, gains, cosv, sinv, cost, sint,
-                 send_sem, recv_sem, own_sem, load_sem, wsem, misc_sem, out_sem):
+                 xv, rbuf, kt_out, vt_out, gath, gath_d, gath_g,
+                 hbuf, qbuf, wbuf, wbuf_d, wl, wl_d, wl_g, gvm, gains, cosv, sinv, cost, sint,
+                 send_sem, recv_sem, own_sem, load_sem, wsem, misc_sem):
     side, seq, dim, ffn = cfg["side"], cfg["seq"], cfg["dim"], cfg["ffn"]
     width, half_w, width_d = cfg["width"], cfg["width"] // 2, cfg["width_d"]
     kv_dim = cfg["kv_dim"]
@@ -212,14 +213,14 @@
         pltpu.make_async_copy(wbuf.at[slot], wbuf.at[slot], wsem.at[slot]).wait()
         return slot
 
+    def down_sem(slot, y):
+        return wsem.at[2 + slot * side + y]
+
     def fetch_down(i):
         slot = lax.rem(i, 2)
-        fetch(gath_d.at[i], wbuf_d.at[slot], wsem.at[2 + slot])
-
-    def wait_down(i):
-        slot = lax.rem(i, 2)
-        pltpu.make_async_copy(wbuf_d.at[slot], wbuf_d.at[slot], wsem.at[2 + slot]).wait()
-        return slot
+        for y in range(side):
+            pltpu.make_async_copy(gath_d.at[i, 0, y], wbuf_d.at[slot, y, :, 0], down_sem(slot, y)).start()
+            pltpu.make_async_copy(gath_d.at[i, 1, :, y], wbuf_d.at[slot, y, :, 1], down_sem(slot, y)).start()
 
     def row_loop(body, block=rb):
         def step(i, carry):
@@ -253,7 +254,6 @@
     head = cfg["head"]
     col_v = (0, n_kv * 128)
     col_k = (2 * n_kv * 128, 2 * n_kv * 128 + seq)
-    col_t = 2 * n_kv * 128 + 2 * seq
 
     def pre(t, carry):
         tick(t)
@@ -288,7 +288,7 @@
         for c in range(kv_dim // 128):
             kr = rope(acc[:, c * 128:(c + 1) * 128], rs)
             kt = jnp.transpose(kr).astype(BF16)
-            rbuf[c * 128:(c + 1) * 128, pl.ds(col_t + rs.start, rs.size)] = kt
+            kt_out[c * 128:(c + 1) * 128, rs] = kt
             zero = jnp.zeros((head, rs.size), BF16)
             for g in range(2):
                 kk = kt[g * head:(g + 1) * head]
@@ -299,7 +299,7 @@
                 rbuf[r0 + head:r0 + 128, pl.ds(col_k[1] + rs.start, rs.size)] = kk
             vv = acc[:, kv_dim + c * 128:kv_dim + (c + 1) * 128]
             vt = jnp.transpose(vv).astype(BF16)
-            rbuf[kv_dim + c * 128:kv_dim + (c + 1) * 128, pl.ds(col_t + rs.start, rs.size)] = vt
+            vt_out[c * 128:(c + 1) * 128, rs] = vt
             turned = pltpu.roll(vv, head, 1)
             g0, g1 = 2 * c, 2 * c + 1
             rbuf[rs, col_v[0] + g0 * 128:col_v[0] + g0 * 128 + 128] = jnp.where(first, vv, 0.0).astype(BF16)
@@ -308,10 +308,6 @@
             rbuf[rs, col_v[1] + g1 * 128:col_v[1] + g1 * 128 + 128] = jnp.where(first, 0.0, vv).astype(BF16)
 
     row_loop(kv_block)
-    kt_out = pltpu.make_async_copy(rbuf.at[pl.ds(0, kv_dim), pl.ds(col_t, seq)], kt_hbm, out_sem.at[n_down])
-    vt_out = pltpu.make_async_copy(rbuf.at[pl.ds(kv_dim, kv_dim), pl.ds(col_t, seq)], vt_hbm, out_sem.at[n_down + 1])
-    kt_out.start()
-    vt_out.start()
 
     def q_step(c, carry):
         tick(READY + 1 + c)
@@ -395,8 +391,6 @@
 
     lax.fori_loop(0, n_o, o_step, 0)
     t_now += n_o
-    kt_out.wait()
-    vt_out.wait()
     norm_rows(xv, qbuf, 8)
 
     ticks_by = [min(j, FFN_PAIRED) // 2 + (j < FFN_PAIRED) + max(0, j - FFN_PAIRED + 1) + (j >= FFN_PAIRED) * (FFN_PAIRED % 2)
@@ -437,45 +431,103 @@
     lax.fori_loop(0, n_ffn, f_step, 0)
     t_now += ticks_by[-1]
 
-    def out_copy(i):
-        cs = pl.ds(pl.multiple_of(i * width_d, width_d), width_d)
-        return pltpu.make_async_copy(xv.at[:, cs], out_hbm.at[:, cs], out_sem.at[i])
+    quarter = ffn // side
 
     def d_step(i, carry):
         tick(t_now + i)
         fetch_down(i)
-        slot = wait_down(i)
+        slot = lax.rem(i, 2)
         cs = pl.ds(pl.multiple_of(i * width_d, width_d), width_d)
 
-        def d_block(rs):
-            acc = jnp.dot(rbuf[rs, :], wbuf_d[slot].reshape(ffn, width_d), preferred_element_type=F32)
+        def add_rows(rs, acc):
             xv[rs, cs] = (xv[rs, cs].astype(F32) + acc.astype(BF16).astype(F32)).astype(BF16)
 
-        row_loop(d_block)
-        out_copy(i).start()
-        return carry
-
-    lax.fori_loop(0, n_down, d_step, 0)
-
-    def finish(i, carry):
-        out_copy(i).wait()
-        return carry
-
-    lax.fori_loop(0, n_down, finish, 0)
+        acc = None
+        for y in range(side):
+            pltpu.make_async_copy(wbuf_d.at[slot, y], wbuf_d.at[slot, y], down_sem(slot, y)).wait()
+            part = jnp.dot(rbuf[0:rb, y * quarter:(y + 1) * quarter], wbuf_d[slot, y].reshape(quarter, width_d),
+                           preferred_element_type=F32)
+            acc = part if acc is None else acc + part
+        add_rows(pl.ds(0, rb), acc)
+
+        def d_rows(k, c2):
+            rs = pl.ds(pl.multiple_of(k * rb, rb), rb)
+            add_rows(rs, jnp.dot(rbuf[rs, :], wbuf_d[slot].reshape(ffn, width_d), preferred_element_type=F32))
+            return c2
+
+        lax.fori_loop(1, seq // rb, d_rows, 0)
+        return carry
+
+    lax.fori_loop(0, n_down - 1, d_step, 0)
+
+    def last_ticks(i, carry):
+        tick(t_now + n_down - 1 + i)
+        return carry
+
+    lax.fori_loop(0, max(1, n_piece + READY - t_now - n_down + 1), last_ticks, 0)
     assert t_now + n_down >= n_piece + READY
 
 
-def copy_kernel(a, b, c, a_out, b_out, c_out):
-    a_out[...] = a[...]
-    b_out[...] = b[...]
-    c_out[...] = c[...]
-
-
-def fresh_copy(a, b, c, steps=4):
-    specs = [pl.BlockSpec((t.shape[0] // steps, t.shape[1]), lambda i: (i, 0)) for t in (a, b, c)]
+def last_kernel(xv, rbuf, kt, vt, gath_d, out_hbm, kt_hbm, vt_hbm, wlast, tail, wsem, sems):
+    seq, dim = xv.shape
+    side = wlast.shape[0]
+    width_d = tail.shape[1]
+    done = dim - width_d
+    last = gath_d.shape[0] - 1
+    rb = min(ROW_BLOCK, seq)
+    for y in range(side):
+        pltpu.make_async_copy(gath_d.at[last, 0, y], wlast.at[y, :, 0], wsem.at[y]).start()
+        pltpu.make_async_copy(gath_d.at[last, 1, :, y], wlast.at[y, :, 1], wsem.at[y]).start()
+    copies = [pltpu.make_async_copy(xv.at[:, pl.ds(0, done)], out_hbm.at[:, pl.ds(0, done)], sems.at[0]),
+              pltpu.make_async_copy(kt, kt_hbm, sems.at[1]), pltpu.make_async_copy(vt, vt_hbm, sems.at[2])]
+    for cp in copies:
+        cp.start()
+
+    def rows_out(i):
+        rs = pl.ds(pl.multiple_of(i * rb, rb), rb)
+        return pltpu.make_async_copy(tail.at[rs], out_hbm.at[rs, pl.ds(done, width_d)], sems.at[3 + i])
+
+    def finish_rows(i, acc):
+        rs = pl.ds(pl.multiple_of(i * rb, rb), rb)
+        tail[rs, :] = (xv[rs, done:].astype(F32) + acc.astype(BF16).astype(F32)).astype(BF16)
+        rows_out(i).start()
+
+    quarter = rbuf.shape[1] // side
+    acc = None
+    for y in range(side):
+        pltpu.make_async_copy(wlast.at[y], wlast.at[y], wsem.at[y]).wait()
+        part = jnp.dot(rbuf[0:rb, y * quarter:(y + 1) * quarter], wlast[y].reshape(quarter, width_d),
+                       preferred_element_type=F32)
+        acc = part if acc is None else acc + part
+    finish_rows(0, acc)
+
+    def block(i, carry):
+        rs = pl.ds(pl.multiple_of(i * rb, rb), rb)
+        finish_rows(i, jnp.dot(rbuf[rs, :], wlast[...].reshape(rbuf.shape[1], width_d), preferred_element_type=F32))
+        return carry
+
+    lax.fori_loop(1, seq // rb, block, 0)
+    for cp in copies:
+        cp.wait()
+    for i in range(seq // rb):
+        rows_out(i).wait()
+
+
+def last_piece(xv, rbuf, kt, vt, gath_d):
+    _, _, side, _, rows_d, width_d = gath_d.shape
+    seq, dim = xv.shape
+    vm, hbm = pl.BlockSpec(memory_space=pltpu.VMEM), pl.BlockSpec(memory_space=pl.ANY)
     return pl.pallas_call(
-        copy_kernel, grid=(steps,), in_specs=specs, out_specs=specs,
-        out_shape=[jax.ShapeDtypeStruct(t.shape, t.dtype) for t in (a, b, c)])(a, b, c)
+        last_kernel, in_specs=[vm] * 4 + [hbm], out_specs=[hbm] * 3,
+        out_shape=[jax.ShapeDtypeStruct(t.shape, t.dtype) for t in (xv, kt, vt)],
+        scratch_shapes=[
+            pltpu.VMEM((side, side, 2, rows_d, width_d), BF16),
+            pltpu.VMEM((seq, width_d), BF16),
+            pltpu.SemaphoreType.DMA((side,)),
+            pltpu.SemaphoreType.DMA((3 + seq // min(ROW_BLOCK, seq),)),
+        ],
+        compiler_params=pltpu.CompilerParams(vmem_limit_bytes=16 << 20),
+    )(xv, rbuf, kt, vt, gath_d)
 
 
 def solution(mesh, width=1024, width_d=256):
@@ -497,8 +549,8 @@
         cfg = dict(side=side, seq=seq, dim=dim, ffn=ffn, width=width, width_d=width_d, kv_dim=kv_dim, q_dim=q_dim,
                    rows=rows, rows_d=rows_d, head=head)
         assert 2 * kv_dim == width and rows == 64 and rows * n_dev == dim
-        both = jnp.stack([g_attn, g_mlp]).astype(F32)
-        gain_tile = jnp.broadcast_to(jnp.pad(both, ((0, 0), (0, 128 - rows)))[:, None, :], (2, 8, 128)).reshape(16, 128)
+        wide = [jnp.pad(g.astype(F32), (0, 128 - rows))[None, :] for g in (g_attn, g_mlp)]
+        gain_tile = jnp.concatenate([jnp.broadcast_to(g, (8, 128)) for g in wide])
         n_wide = (2 * kv_dim + q_dim + dim + 2 * ffn) // width
         n_down = dim // width_d
         n_piece = n_wide + n_down
@@ -506,19 +558,18 @@
         res = pl.pallas_call(
             functools.partial(layer_kernel, cfg),
             out_shape=(
-                jax.ShapeDtypeStruct((seq, dim), BF16),
-                jax.ShapeDtypeStruct((kv_dim, seq), BF16),
-                jax.ShapeDtypeStruct((kv_dim, seq), BF16),
+                pltpu.VMEM((seq, dim), BF16),
+                pltpu.VMEM((max(seq, 2 * kv_dim), ffn), BF16),
+                pltpu.VMEM((kv_dim, seq), BF16),
+                pltpu.VMEM((kv_dim, seq), BF16),
                 jax.ShapeDtypeStruct((n_wide, 2, side, side, rows, width), BF16),
                 jax.ShapeDtypeStruct((n_down, 2, side, side, rows_d, width_d), BF16),
                 jax.ShapeDtypeStruct((2, side, side, 16, 128), F32)),
             in_specs=[hbm] * 11,
-            out_specs=[hbm] * 6,
+            out_specs=[pl.BlockSpec(memory_space=pltpu.VMEM)] * 4 + [hbm] * 3,
             scratch_shapes=[
-                pltpu.VMEM((seq, dim), BF16),
                 pltpu.VMEM((seq, max(dim, q_dim)), BF16),
                 pltpu.VMEM((seq, max(dim, q_dim)), BF16),
-                pltpu.VMEM((max(seq, 2 * kv_dim), ffn), BF16),
                 pltpu.VMEM((2, side, side, 2, rows, width), BF16),
                 pltpu.VMEM((2, side, side, 2, rows_d, width_d), BF16),
                 pltpu.VMEM((n_wide, rows, width), BF16),
@@ -534,14 +585,13 @@
                 pltpu.SemaphoreType.DMA((6, 2, SLOTS + 1)),
                 pltpu.SemaphoreType.DMA((SLOTS + 1,)),
                 pltpu.SemaphoreType.DMA((n_piece + 1,)),
-                pltpu.SemaphoreType.DMA((4,)),
+                pltpu.SemaphoreType.DMA((2 + 2 * side,)),
                 pltpu.SemaphoreType.DMA((3,)),
-                pltpu.SemaphoreType.DMA((n_down + 2,)),
             ],
             compiler_params=pltpu.CompilerParams(
-                collective_id=0, has_side_effects=True, vmem_limit_bytes=67043328),
+                collective_id=0, has_side_effects=True, vmem_limit_bytes=VMEM_MAIN),
         )(hidden[0], gain_tile, w_query, w_key, w_value, w_out, w_gate, w_up, w_down, cos_tab.T, sin_tab.T)
-        out, kt, vt = fresh_copy(*res[:3])
+        out, kt, vt = last_piece(*res[:4], res[5])
 
         def cache(t):
             return jnp.transpose(t.reshape(1, kv_dim // head, head, seq), (0, 3, 1, 2))

time: 352 us -> 350 us (level)
  no operation moved by 1% of the time
where the time goes in v4:
time: 350 us
  Pallas kernels  347 us (99%)
    pallas_call x1, Pallas kernels, local_layer(): pl.pallas_call(functools.partial(layer_kernel, cfg), out_shape=(pltpu.VME...  337 us
    pallas_call x1, Pallas kernels, last_piece(): pl.pallas_call(last_kernel, in_specs=[vm] * 4 + [hbm], out_specs=[hbm] *...  10 us

profile of v4, /device:TPU:97, one launch (start us, length us, event | category | flops | bytes accessed | tf_op | source)
XLA Modules:
  0.0 350.1 jit_solution(15439810126180220694)
XLA Ops:
  0.6 0.7 pad_convert_fusion.1
  1.3 0.7 pad_convert_fusion
  2.0 0.6 pad_maximum_fusion.gain_hbm
  2.6 337.3 %shard_map.139 = (bf16[1024,2048]{1,0:T(8,128)(2,1)S(1)}, bf16[1024,8192]{1,0:T(8,128)(2,1)S(1)}, bf16[512,1024]{1,0:T(8,128)(2,1)S(1)}, bf16[512,1024]{1,0:T(8,...) custom-call(bf16[1024,2048]{1,0:T(8,128)(2,1)} %bitcast.10, ...), custom_call_target="tpu_custom_call" | custom-call | tf_op jit(solution)/shard_map/pallas_call | solution.py:558
  339.9 10.0 %shard_map.140 = (bf16[1024,2048]{1,0:T(8,128)(2,1)}, bf16[512,1024]{1,0:T(8,128)(2,1)}, bf16[512,1024]{1,0:T(8,128)(2,1)}) custom-call(bf16[1024,2048]{1,0:T(8,128)(2,1)S(1)} %get-tuple-element.11.xv, bf16[1024,8192]{1,0:T(8,128)(2,1)S(1)} %get-tuple-element.12.rbuf, bf16[512,1024]{1,0:T(8,128)(2,1)S(1)} %get-tuple-element.13.kt, ...), custom_call_target="tpu_custom_call" | custom-call | tf_op jit(solution)/shard_map/pallas_call | solution.py:520
  (2 shorter events, 0.0 us)

commit v5 on v4

--- a/solution.py
+++ b/solution.py
@@ -21,7 +21,7 @@
 
 
 def layer_kernel(cfg, x_hbm, gain_hbm, wq, wk, wv, wo, wg, wu, wd, cos_hbm, sin_hbm,
-                 xv, rbuf, kt_out, vt_out, gath, gath_d, gath_g,
+                 xv, rbuf, kt_out, vt_out, accv, gath, gath_d, gath_g,
                  hbuf, qbuf, wbuf, wbuf_d, wl, wl_d, wl_g, gvm, gains, cosv, sinv, cost, sint,
                  send_sem, recv_sem, own_sem, load_sem, wsem, misc_sem):
     side, seq, dim, ffn = cfg["side"], cfg["seq"], cfg["dim"], cfg["ffn"]
@@ -213,14 +213,15 @@
         pltpu.make_async_copy(wbuf.at[slot], wbuf.at[slot], wsem.at[slot]).wait()
         return slot
 
-    def down_sem(slot, y):
-        return wsem.at[2 + slot * side + y]
-
-    def fetch_down(i):
+    half = ffn // 2
+
+    def down_copy(i, c, which):
         slot = lax.rem(i, 2)
-        for y in range(side):
-            pltpu.make_async_copy(gath_d.at[i, 0, y], wbuf_d.at[slot, y, :, 0], down_sem(slot, y)).start()
-            pltpu.make_async_copy(gath_d.at[i, 1, :, y], wbuf_d.at[slot, y, :, 1], down_sem(slot, y)).start()
+        return pltpu.make_async_copy(gath_d.at[i, c], wbuf_d.at[slot, c], wsem.at[2 + slot * 2 + which])
+
+    def down_dot(i, c, rs):
+        lhs = rbuf[rs, pl.ds(pl.multiple_of(c * half, 128), half)]
+        return jnp.dot(lhs, wbuf_d[lax.rem(i, 2), c].reshape(half, width_d), preferred_element_type=F32)
 
     def row_loop(body, block=rb):
         def step(i, carry):
@@ -422,8 +423,10 @@
             acc = jnp.dot(qbuf[rs, :], weight(slot), preferred_element_type=F32)
             gate = acc[:, :half_w].astype(BF16).astype(F32)
             up = acc[:, half_w:].astype(BF16).astype(F32)
-            cs = pl.ds(pl.multiple_of(j * half_w, half_w), half_w)
-            rbuf[rs, cs] = (jax.nn.silu(gate) * up).astype(BF16)
+            act = (jax.nn.silu(gate) * up).astype(BF16)
+            chip_t = lax.rem(j, side) * side + j // side
+            rbuf[rs, pl.ds(pl.multiple_of(j * rows_d, 128), rows_d)] = act[:, :rows_d]
+            rbuf[rs, pl.ds(pl.multiple_of(half + chip_t * rows_d, 128), rows_d)] = act[:, rows_d:]
 
         row_loop(f_block)
         return carry
@@ -431,57 +434,56 @@
     lax.fori_loop(0, n_ffn, f_step, 0)
     t_now += ticks_by[-1]
 
-    quarter = ffn // side
+    def own_half(i):
+        down_copy(i, core, 0).wait()
+
+        def rows_own(rs):
+            accv[rs, :] = down_dot(i, core, rs)
+
+        row_loop(rows_own)
+
+    down_copy(0, core, 0).start()
 
     def d_step(i, carry):
         tick(t_now + i)
-        fetch_down(i)
-        slot = lax.rem(i, 2)
+        down_copy(i, 1 - core, 1).start()
+        down_copy(i + 1, core, 0).start()
+        own_half(i)
+        down_copy(i, 1 - core, 1).wait()
         cs = pl.ds(pl.multiple_of(i * width_d, width_d), width_d)
 
-        def add_rows(rs, acc):
+        def rows_rest(rs):
+            acc = accv[rs, :] + down_dot(i, 1 - core, rs)
             xv[rs, cs] = (xv[rs, cs].astype(F32) + acc.astype(BF16).astype(F32)).astype(BF16)
 
-        acc = None
-        for y in range(side):
-            pltpu.make_async_copy(wbuf_d.at[slot, y], wbuf_d.at[slot, y], down_sem(slot, y)).wait()
-            part = jnp.dot(rbuf[0:rb, y * quarter:(y + 1) * quarter], wbuf_d[slot, y].reshape(quarter, width_d),
-                           preferred_element_type=F32)
-            acc = part if acc is None else acc + part
-        add_rows(pl.ds(0, rb), acc)
-
-        def d_rows(k, c2):
-            rs = pl.ds(pl.multiple_of(k * rb, rb), rb)
-            add_rows(rs, jnp.dot(rbuf[rs, :], wbuf_d[slot].reshape(ffn, width_d), preferred_element_type=F32))
-            return c2
-
-        lax.fori_loop(1, seq // rb, d_rows, 0)
+        row_loop(rows_rest)
         return carry
 
     lax.fori_loop(0, n_down - 1, d_step, 0)
+    own_half(n_down - 1)
 
     def last_ticks(i, carry):
         tick(t_now + n_down - 1 + i)
         return carry
 
     lax.fori_loop(0, max(1, n_piece + READY - t_now - n_down + 1), last_ticks, 0)
-    assert t_now + n_down >= n_piece + READY
-
-
-def last_kernel(xv, rbuf, kt, vt, gath_d, out_hbm, kt_hbm, vt_hbm, wlast, tail, wsem, sems):
+    assert t_now + n_down >= n_piece + READY and t_now - 1 - 4 * LAG >= first_d and half_w == 2 * rows_d
+
+
+def last_kernel(xv, rbuf, kt, vt, accv, gath_d, out_hbm, kt_hbm, vt_hbm, wlast, tail, wsem, sems):
     seq, dim = xv.shape
-    side = wlast.shape[0]
-    width_d = tail.shape[1]
+    side, _, rows_d, width_d = wlast.shape
     done = dim - width_d
     last = gath_d.shape[0] - 1
     rb = min(ROW_BLOCK, seq)
-    for y in range(side):
-        pltpu.make_async_copy(gath_d.at[last, 0, y], wlast.at[y, :, 0], wsem.at[y]).start()
-        pltpu.make_async_copy(gath_d.at[last, 1, :, y], wlast.at[y, :, 1], wsem.at[y]).start()
+    part_k = side * rows_d
+    other = 1 - lax.rem(lax.axis_index("fsdp"), 2)
+    base = other * (rbuf.shape[1] // 2)
+    parts = [pltpu.make_async_copy(gath_d.at[last, other, b], wlast.at[b], wsem.at[b]) for b in range(side)]
+    for cp in parts:
+        cp.start()
     copies = [pltpu.make_async_copy(xv.at[:, pl.ds(0, done)], out_hbm.at[:, pl.ds(0, done)], sems.at[0]),
               pltpu.make_async_copy(kt, kt_hbm, sems.at[1]), pltpu.make_async_copy(vt, vt_hbm, sems.at[2])]
-    for cp in copies:
-        cp.start()
 
     def rows_out(i):
         rs = pl.ds(pl.multiple_of(i * rb, rb), rb)
@@ -489,21 +491,23 @@
 
     def finish_rows(i, acc):
         rs = pl.ds(pl.multiple_of(i * rb, rb), rb)
+        acc = accv[rs, :] + acc
         tail[rs, :] = (xv[rs, done:].astype(F32) + acc.astype(BF16).astype(F32)).astype(BF16)
         rows_out(i).start()
 
-    quarter = rbuf.shape[1] // side
     acc = None
-    for y in range(side):
-        pltpu.make_async_copy(wlast.at[y], wlast.at[y], wsem.at[y]).wait()
-        part = jnp.dot(rbuf[0:rb, y * quarter:(y + 1) * quarter], wlast[y].reshape(quarter, width_d),
-                       preferred_element_type=F32)
+    for b in range(side):
+        parts[b].wait()
+        lhs = rbuf[0:rb, pl.ds(pl.multiple_of(base + b * part_k, 128), part_k)]
+        part = jnp.dot(lhs, wlast[b].reshape(part_k, width_d), preferred_element_type=F32)
         acc = part if acc is None else acc + part
+    for cp in copies:
+        cp.start()
     finish_rows(0, acc)
 
     def block(i, carry):
-        rs = pl.ds(pl.multiple_of(i * rb, rb), rb)
-        finish_rows(i, jnp.dot(rbuf[rs, :], wlast[...].reshape(rbuf.shape[1], width_d), preferred_element_type=F32))
+        lhs = rbuf[pl.ds(pl.multiple_of(i * rb, rb), rb), pl.ds(pl.multiple_of(base, 128), side * part_k)]
+        finish_rows(i, jnp.dot(lhs, wlast[...].reshape(side * part_k, width_d), preferred_element_type=F32))
         return carry
 
     lax.fori_loop(1, seq // rb, block, 0)
@@ -513,21 +517,21 @@
         rows_out(i).wait()
 
 
-def last_piece(xv, rbuf, kt, vt, gath_d):
+def last_piece(xv, rbuf, kt, vt, accv, gath_d):
     _, _, side, _, rows_d, width_d = gath_d.shape
     seq, dim = xv.shape
     vm, hbm = pl.BlockSpec(memory_space=pltpu.VMEM), pl.BlockSpec(memory_space=pl.ANY)
     return pl.pallas_call(
-        last_kernel, in_specs=[vm] * 4 + [hbm], out_specs=[hbm] * 3,
+        last_kernel, in_specs=[vm] * 5 + [hbm], out_specs=[hbm] * 3,
         out_shape=[jax.ShapeDtypeStruct(t.shape, t.dtype) for t in (xv, kt, vt)],
         scratch_shapes=[
-            pltpu.VMEM((side, side, 2, rows_d, width_d), BF16),
+            pltpu.VMEM((side, side, rows_d, width_d), BF16),
             pltpu.VMEM((seq, width_d), BF16),
             pltpu.SemaphoreType.DMA((side,)),
             pltpu.SemaphoreType.DMA((3 + seq // min(ROW_BLOCK, seq),)),
         ],
         compiler_params=pltpu.CompilerParams(vmem_limit_bytes=16 << 20),
-    )(xv, rbuf, kt, vt, gath_d)
+    )(xv, rbuf, kt, vt, accv, gath_d)
 
 
 def solution(mesh, width=1024, width_d=256):
@@ -549,8 +553,8 @@
         cfg = dict(side=side, seq=seq, dim=dim, ffn=ffn, width=width, width_d=width_d, kv_dim=kv_dim, q_dim=q_dim,
                    rows=rows, rows_d=rows_d, head=head)
         assert 2 * kv_dim == width and rows == 64 and rows * n_dev == dim
-        wide = [jnp.pad(g.astype(F32), (0, 128 - rows))[None, :] for g in (g_attn, g_mlp)]
-        gain_tile = jnp.concatenate([jnp.broadcast_to(g, (8, 128)) for g in wide])
+        both = jnp.stack([g_attn, g_mlp]).astype(F32)
+        gain_tile = jnp.broadcast_to(jnp.pad(both, ((0, 0), (0, 128 - rows)))[:, None, :], (2, 8, 128)).reshape(16, 128)
         n_wide = (2 * kv_dim + q_dim + dim + 2 * ffn) // width
         n_down = dim // width_d
         n_piece = n_wide + n_down
@@ -562,16 +566,17 @@
                 pltpu.VMEM((max(seq, 2 * kv_dim), ffn), BF16),
                 pltpu.VMEM((kv_dim, seq), BF16),
                 pltpu.VMEM((kv_dim, seq), BF16),
+                pltpu.VMEM((seq, width_d), F32),
                 jax.ShapeDtypeStruct((n_wide, 2, side, side, rows, width), BF16),
                 jax.ShapeDtypeStruct((n_down, 2, side, side, rows_d, width_d), BF16),
                 jax.ShapeDtypeStruct((2, side, side, 16, 128), F32)),
             in_specs=[hbm] * 11,
-            out_specs=[pl.BlockSpec(memory_space=pltpu.VMEM)] * 4 + [hbm] * 3,
+            out_specs=[pl.BlockSpec(memory_space=pltpu.VMEM)] * 5 + [hbm] * 3,
             scratch_shapes=[
                 pltpu.VMEM((seq, max(dim, q_dim)), BF16),
                 pltpu.VMEM((seq, max(dim, q_dim)), BF16),
                 pltpu.VMEM((2, side, side, 2, rows, width), BF16),
-                pltpu.VMEM((2, side, side, 2, rows_d, width_d), BF16),
+                pltpu.VMEM((2, 2, side, side, rows_d, width_d), BF16),
                 pltpu.VMEM((n_wide, rows, width), BF16),
                 pltpu.VMEM((n_down, rows_d, width_d), BF16),
                 pltpu.VMEM((16, 128), F32),
@@ -585,13 +590,13 @@
                 pltpu.SemaphoreType.DMA((6, 2, SLOTS + 1)),
                 pltpu.SemaphoreType.DMA((SLOTS + 1,)),
                 pltpu.SemaphoreType.DMA((n_piece + 1,)),
-                pltpu.SemaphoreType.DMA((2 + 2 * side,)),
+                pltpu.SemaphoreType.DMA((6,)),
                 pltpu.SemaphoreType.DMA((3,)),
             ],
             compiler_params=pltpu.CompilerParams(
                 collective_id=0, has_side_effects=True, vmem_limit_bytes=VMEM_MAIN),
         )(hidden[0], gain_tile, w_query, w_key, w_value, w_out, w_gate, w_up, w_down, cos_tab.T, sin_tab.T)
-        out, kt, vt = last_piece(*res[:4], res[5])
+        out, kt, vt = last_piece(*res[:5], res[6])
 
         def cache(t):
             return jnp.transpose(t.reshape(1, kv_dim // head, head, seq), (0, 3, 1, 2))

time: 350 us -> 346 us (0.989)
  Pallas kernels: 347 us -> 339 us
  local copies, waits for them, and re-layouts: 0.01 us -> 4.8 us
    pallas_call x1, Pallas kernels: 10 us -> 5.51 us  [last_piece(): pl.pallas_call(last_kernel, in_specs=[vm] * 5 + [hbm], out_specs=[hbm] *...]
    unnamed x0 -> x4, local copies, waits for them, and re-layouts: none -> 4.2 us
where the time goes in v5:
time: 346 us
  Pallas kernels  339 us (98%)
  local copies, waits for them, and re-layouts  4.8 us (1%)
    pallas_call x1, Pallas kernels, local_layer(): pl.pallas_call(functools.partial(layer_kernel, cfg), out_shape=(pltpu.VME...  334 us

profile of v5, /device:TPU:97, one launch (start us, length us, event | category | flops | bytes accessed | tf_op | source)
XLA Modules:
  0.0 345.7 jit_solution(1027063423188976899)
XLA Ops:
  0.6 0.7 fusion.3
  1.3 0.6 broadcast_bitcast_fusion.gain_hbm
  1.9 333.9 %shard_map.139 = (bf16[1024,2048]{1,0:T(8,128)(2,1)S(1)}, bf16[1024,8192]{1,0:T(8,128)(2,1)S(1)}, bf16[512,1024]{1,0:T(8,128)(2,1)S(1)}, bf16[512,1024]{1,0:T(8,...) custom-call(bf16[1024,2048]{1,0:T(8,128)(2,1)} %bitcast.14, ...), custom_call_target="tpu_custom_call" | custom-call | tf_op jit(solution)/shard_map/pallas_call | solution.py:562
  335.8 0.0 copy-start
  335.9 2.0 copy-done
  337.9 0.0 copy-start.1
  337.9 2.2 copy-done.1
  340.1 5.5 %shard_map.140 = (bf16[1024,2048]{1,0:T(8,128)(2,1)}, bf16[512,1024]{1,0:T(8,128)(2,1)}, bf16[512,1024]{1,0:T(8,128)(2,1)}) custom-call(bf16[1024,2048]{1,0:T(8,128)(2,1)S(1)} %copy-done.1, bf16[1024,8192]{1,0:T(8,128)(2,1)S(1)} %get-tuple-element.13.rbuf, bf16[512,1024]{1,0:T(8,128)(2,1)S(1)} %get-tuple-element.14.kt, ...), custom_call_target="tpu_custom_call" | custom-call | tf_op jit(solution)/shard_map/pallas_call | solution.py:524
Async XLA Ops:
  335.8 2.0 copy-start
  337.9 2.2 copy-start.1
